TPU v7x, 256 devices: a whole 4x4x8 slice. The times are simulated.
256 devices in a mesh: dp: 2 (over core), section: 8 (over z), mp: 16 (over y, x).
Axes of the slice: x: 4, y: 4, z: 8, core: 2. Of those that a mesh axis runs over, the one named last changes fastest.
Arguments:
- inputs: bfloat16 [192, 512], P(('dp', 'mp')), may hold values from -6 to 6
- tangents: bfloat16 [192, 32, 512], P(('dp', 'mp')), may hold values from -6 to 6
- targets: bfloat16 [192, 1024], P(('dp', 'mp')), may hold values from -24 to 24
- target_jac: bfloat16 [192, 32, 1024], P(('dp', 'mp')), may hold values from -24 to 24
- rank_mask: int32 [192, 32], P(('dp', 'mp')), may hold values from 0 to 1, as said below
- batch_order: int32 [32, 6], P(('dp', 'mp')), may hold values from 0 to 5, each once within a row
- encoder: bfloat16 [512, 2048], replicated, may hold values from -0.25 to 0.25
- layers: bfloat16 [8, 2048, 2048], P('section', 'mp'), may hold values from -0.125 to 0.125
- head_weight: bfloat16 [2048, 1024], replicated, may hold values from -0.125 to 0.125
Outputs:
- grad_layers: float32 [8, 2048, 2048], P('section', ('dp', 'mp'))
- grad_head: float32 [2048, 1024], P(('dp', 'mp'), 'section')
- loss_value: float32 [], replicated
Inputs may be any that keep to these rules, and one draw needn't show every extreme that they name: `rank_mask`: each sample's ones are its first 1 to 32 directions. `batch_order`: each row is an ordering of 0 .. 5.
All inputs are finite; a program needn't handle non-finite values.
Results may differ from a plain program's by a relative error of at most 0.035.
Values may be sent and summed in bfloat16 or wider, within the bound.
A program may use at most 128 MiB of HBM per device.

v0:
```python
import jax
import jax.numpy as jnp
from jax import lax
from jax.sharding import PartitionSpec as P

MB = 6


def from_behind(value, axis, steps):
    count = lax.axis_size(axis)
    initial, last = (max(0, -steps), min(count, count - steps))
    return lax.ppermute(value, axis, [(source, source + steps) for source in range(initial, last)])


def in_blocks(array, dim, count):
    before, after = (array.shape[:dim], array.shape[dim + 1 :])
    return jnp.moveaxis(array.reshape(*before, count, -1, *after), dim, 0)


def sent_and_summed(array, axis, dim):
    parts = in_blocks(array, dim, lax.axis_size(axis))
    arrived = lax.all_to_all(parts, axis, split_axis=0, concat_axis=0, tiled=True)
    return arrived.astype(jnp.float32).sum(axis=0)


def from_everyone(array, axis):
    count = lax.axis_size(axis)
    return lax.all_to_all(
        jnp.broadcast_to(array[None], (count, *array.shape)), axis, 0, 0, tiled=True
    )


def over_copies(array, axis):
    return from_everyone(array, axis).sum(axis=0)


def forward_layer(row_block, weight):
    model_width = weight.shape[1]
    pre_act = jnp.dot(
        row_block.reshape(-1, model_width), weight, preferred_element_type=jnp.float32
    ).reshape(row_block.shape)
    tanh_p = jnp.tanh(pre_act[:, 0])
    slope_vals = 1.0 - tanh_p * tanh_p
    primal = row_block[:, 0].astype(jnp.float32) + tanh_p
    tangent = row_block[:, 1:].astype(jnp.float32) + slope_vals[:, None, :] * pre_act[:, 1:]
    return (jnp.concatenate([primal[:, None], tangent], axis=1).astype(jnp.bfloat16), pre_act)


def backward_layer(pre_act, grad_rows, weight):
    model_width = weight.shape[1]
    upstream = grad_rows.astype(jnp.float32)
    tanh_p = jnp.tanh(pre_act[:, 0])
    slope_vals = 1.0 - tanh_p * tanh_p
    tangent_part = upstream[:, 1:] * slope_vals[:, None, :]
    slope_grad = jnp.sum(upstream[:, 1:] * pre_act[:, 1:], axis=1)
    primal_part = upstream[:, 0] * slope_vals - 2.0 * slope_grad * tanh_p * slope_vals
    grad_mix = jnp.concatenate([primal_part[:, None], tangent_part], axis=1).astype(jnp.bfloat16)
    back_rows = jnp.dot(
        grad_mix.reshape(-1, model_width), weight.T, preferred_element_type=jnp.float32
    ).reshape(upstream.shape)
    return (grad_mix, (upstream + back_rows).astype(jnp.bfloat16))


def place_slot(store, value, batch_slot, is_valid):
    return lax.dynamic_update_index_in_dim(
        store, jnp.where(is_valid, value, store[batch_slot]), batch_slot, 0
    )


def local(
    inputs, tangents, targets, target_jac, rank_mask, batch_order, encoder, layers, head_weight
):
    samp_dev = inputs.shape[0]
    per_batch = samp_dev // MB
    row_depth = tangents.shape[1] + 1
    in_width = inputs.shape[1]
    model_width = layers.shape[2]
    out_width = head_weight.shape[1]
    sections = lax.axis_size("section")
    section_id = lax.axis_index("section")
    is_first = section_id == 0
    is_last = section_id == sections - 1
    layer_full = lax.all_gather(layers[0], "mp", axis=0, tiled=True)
    sample_order = batch_order[0]
    row_weight = jnp.concatenate(
        [jnp.ones((samp_dev, 1), jnp.float32), rank_mask.astype(jnp.float32)], axis=1
    )
    sample_total = jnp.sum(row_weight, axis=1)
    batch_counts = lax.psum(
        jnp.sum(sample_total[sample_order].reshape(MB, per_batch), axis=1), "mp"
    )

    def picked_of(batch_slot):
        return lax.dynamic_slice_in_dim(sample_order, batch_slot * per_batch, per_batch)

    def lift_batch(batch_slot):
        picked = picked_of(batch_slot)
        rows_in = jnp.concatenate([inputs[picked][:, None, :], tangents[picked]], axis=1)
        lifted = jnp.dot(rows_in.reshape(-1, in_width), encoder, preferred_element_type=jnp.float32)
        return lifted.reshape(per_batch, row_depth, model_width).astype(jnp.bfloat16)

    block_shape = (MB, per_batch, row_depth, model_width)
    pre_shape = (1, 1, 1, 1)

    def forward_tick(step_index, loop_state):
        incoming, store_in, store_pre, store_out = loop_state
        batch_index = step_index - section_id
        is_valid = (batch_index >= 0) & (batch_index < MB)
        batch_slot = jnp.clip(batch_index, 0, MB - 1)
        row_block = lax.cond(is_first, lambda: lift_batch(batch_slot), lambda: incoming)

        def forward_active():
            return forward_layer(row_block, layer_full)

        def forward_resting():
            return (row_block, jnp.zeros(row_block.shape, jnp.float32))

        layer_out, pre_act = lax.cond(is_valid, forward_active, forward_resting)
        store_in = place_slot(store_in, row_block, batch_slot, is_valid)
        store_out = place_slot(store_out, layer_out, batch_slot, is_valid)
        passed = from_behind(layer_out, "section", 1)
        return (passed, store_in, store_pre, store_out)

    start_state = (
        jnp.zeros(block_shape[1:], jnp.bfloat16),
        jnp.zeros(block_shape, jnp.bfloat16),
        jnp.zeros(pre_shape, jnp.float32),
        jnp.zeros(block_shape, jnp.bfloat16),
    )
    _, store_in, store_pre, store_out = lax.fori_loop(
        0, MB + sections - 1, forward_tick, start_state
    )

    def backward_tick(step_index, loop_state):
        incoming, store_mix, store_head, loss_acc = loop_state
        batch_index = step_index - (sections - 1 - section_id)
        is_valid = (batch_index >= 0) & (batch_index < MB)
        batch_slot = jnp.clip(batch_index, 0, MB - 1)
        batch_total = batch_counts[batch_slot]

        def head_part():
            final_rows = store_out[batch_slot]
            outputs = jnp.dot(
                final_rows.reshape(-1, model_width), head_weight, preferred_element_type=jnp.float32
            )
            outputs = outputs.reshape(per_batch, row_depth, out_width)
            picked = picked_of(batch_slot)
            wanted = jnp.concatenate(
                [targets[picked][:, None, :], target_jac[picked]], axis=1
            ).astype(jnp.float32)
            weights_here = row_weight[picked]
            mismatch = outputs - wanted
            misfit = jnp.sum(weights_here[:, :, None] * mismatch * mismatch) / batch_total
            cot_out = (2.0 * weights_here[:, :, None] * mismatch / batch_total).astype(jnp.bfloat16)
            grad_rows = jnp.dot(
                cot_out.reshape(-1, out_width), head_weight.T, preferred_element_type=jnp.float32
            )
            return (
                grad_rows.reshape(per_batch, row_depth, model_width).astype(jnp.bfloat16),
                cot_out,
                misfit,
            )

        def pass_on():
            return (
                incoming,
                jnp.zeros((per_batch, row_depth, out_width), jnp.bfloat16),
                jnp.zeros((), jnp.float32),
            )

        grad_rows, cot_out, misfit = lax.cond(is_last & is_valid, head_part, pass_on)

        def backward_active():
            row_block = store_in[batch_slot]
            pre_act = jnp.dot(
                row_block.reshape(-1, model_width), layer_full, preferred_element_type=jnp.float32
            ).reshape(row_block.shape)
            return backward_layer(pre_act, grad_rows, layer_full)

        def backward_resting():
            return (jnp.zeros(grad_rows.shape, jnp.bfloat16), grad_rows)

        grad_mix, grad_in = lax.cond(is_valid, backward_active, backward_resting)
        store_mix = place_slot(store_mix, grad_mix, batch_slot, is_valid)
        store_head = place_slot(store_head, cot_out, batch_slot, is_valid)
        loss_acc = loss_acc + jnp.where(is_valid, misfit, jnp.zeros((), jnp.float32))
        passed = from_behind(grad_in, "section", -1)
        return (passed, store_mix, store_head, loss_acc)

    back_state = (
        jnp.zeros(block_shape[1:], jnp.bfloat16),
        jnp.zeros(block_shape, jnp.bfloat16),
        jnp.zeros((MB, per_batch, row_depth, out_width), jnp.bfloat16),
        jnp.zeros((), jnp.float32),
    )
    _, store_mix, store_head, loss_acc = lax.fori_loop(
        0, MB + sections - 1, backward_tick, back_state
    )
    shard_rows = model_width // (lax.axis_size("dp") * lax.axis_size("mp"))
    in_flat = store_in.reshape(-1, model_width)
    mix_flat = store_mix.reshape(-1, model_width)
    grad_layers = lax.psum_scatter(
        jnp.dot(in_flat.T, mix_flat, preferred_element_type=jnp.float32).astype(jnp.bfloat16),
        ("dp", "mp"),
        scatter_dimension=0,
        tiled=True,
    ).astype(jnp.float32)[None]
    out_flat = store_out.reshape(-1, model_width)
    head_flat = store_head.reshape(-1, out_width)

    def compute():
        return jnp.dot(out_flat.T, head_flat, preferred_element_type=jnp.float32)

    def skipped():
        return jnp.zeros((shard_rows * lax.axis_size(("dp", "mp")), out_width), jnp.float32)

    summed = sent_and_summed(
        lax.cond(is_last, compute, skipped).astype(jnp.bfloat16), ("dp", "mp"), 0
    )
    section_loss = over_copies(loss_acc, ("dp", "mp"))
    loss_row = jnp.broadcast_to(section_loss, (1, sections))
    grad_head, loss_cols = (
        sent_and_summed(summed.astype(jnp.bfloat16), "section", 1),
        sent_and_summed(loss_row.astype(jnp.bfloat16), "section", 1),
    )
    loss_value = loss_cols[0, 0] / (lax.axis_size("dp") * MB * out_width)
    return (grad_layers, grad_head, loss_value)


def solution(mesh):
    in_specs = (
        P(("dp", "mp"), None),
        P(("dp", "mp"), None, None),
        P(("dp", "mp"), None),
        P(("dp", "mp"), None, None),
        P(("dp", "mp"), None),
        P(("dp", "mp"), None),
        P(),
        P("section", "mp", None),
        P(),
    )
    out_specs = (P("section", ("dp", "mp"), None), P(("dp", "mp"), "section"), P())
    return jax.shard_map(local, mesh=mesh, in_specs=in_specs, out_specs=out_specs, check_vma=False)
```

profile of v0, /device:TPU:1, one launch (start us, length us, event | category | flops | bytes accessed | tf_op | source)
XLA Modules:
  0.0 672.0 jit_solution(17826597853342746980)
XLA Ops:
  10.1 34.4 %psum.7 = f32[6]{0:T(128)S(1)} all-reduce(f32[6]{0:T(128)S(1)} %gather_fusion), channel_id=1, replica_groups=mesh['dp'=2,'section'=8,'mp'=16] {'mp'}, use_global_device_ids=true, to_apply=%region_7.0 | all-reduce | flops 6 | bytes 48 | tf_op jit(solution)/shard_map/psum | solution.py:89
  44.5 45.4 %all-gather.3.cloned.1.call-done = bf16[1,2048,2048]{2,1,0:T(8,128)(2,1)} async-done(((bf16[1,128,2048]{2,1,0:T(8,128)(2,1)}), bf16[1,2048,2048]{2,1,0:T(8,128)(2,1)}) %all-gather.3.cloned.1.call-update) | async-done | bytes 8388624 | tf_op jit(solution)/shard_map/all_gather | solution.py:83
  90.1 166.5 %while.49 = (s32[]{:T(128)}, bf16[1,33,2048]{2,1,0:T(8,128)(2,1)S(1)}, bf16[6,1,33,2048]{3,2,1,0:T(8,128)(2,1)S(1)}, bf16[6,1,33,2048]{3,2,1,0:T(8,128)(2,1)S(1)...) while((s32[]{:T(128)}, ...), condition=%wide.region_5.0_spmd, body=%wide.region_0.5_spmd.sunk | while | flops 346843136 | bytes 14290341 | solution.py:130
  121.7 6.7 conditional.10
  137.1 6.7 conditional.10
  152.6 6.7 conditional.10
  183.4 6.7 conditional.10
  205.0 6.7 conditional.10
  257.8 264.7 %while.50 = (s32[]{:T(128)}, bf16[1,33,2048]{2,1,0:T(8,128)(2,1)S(1)}, bf16[6,1,33,2048]{3,2,1,0:T(8,128)(2,1)}, bf16[6,1,33,1024]{3,2,1,0:T(8,128)(2,1)S(1)}, f...) while((s32[]{:T(128)}, ...), condition=%wide.region_15.16_spmd, body=%wide.region_8.15_spmd.sunk | while | flops 832231424 | bytes 80654912 | solution.py:196
  303.8 71.5 %collective-permute-done.1 = bf16[1,33,2048]{2,1,0:T(8,128)(2,1)S(1)} collective-permute-done((bf16[1,33,2048]{2,1,0:T(8,128)(2,1)S(1)}, bf16[1,33,2048]{2,1,0:T(8,128)(2,1)S(1)}, u32[]{:S(2)}, u32[]{:S(2)}) %collective-permute-start.1) | collective-permute-done | bytes 135200 | tf_op jit(solution)/shard_map/while/body/eval_jaxpr/ppermute | solution.py:12
  375.9 8.5 %conditional.13 = (bf16[1,33,2048]{2,1,0:T(8,128)(2,1)S(1)}, bf16[1,33,2048]{2,1,0:T(8,128)(2,1)S(1)}) conditional(s32[]{:T(128)} %convert_element_type.144, bf16[1,33,2048]{2,1,0:T(8,128)(2,1)S(1)} %get-tuple-element.973, (bf16[1,33,2048]{2,1,0:T(8,128)(2,1)S(1)}, s32[]{:T(128)}, bf16[6,1,33,2048]{3,2,1,0:T(8,128)(2,1)S(1)}, ...), branch_computations={%region_12.12_spmd, %region_13.14_spmd} | conditional | flops 554866688 | bytes 53235792 | solution.py:183
  388.3 13.4 %collective-permute-done.1 = bf16[1,33,2048]{2,1,0:T(8,128)(2,1)S(1)} collective-permute-done((bf16[1,33,2048]{2,1,0:T(8,128)(2,1)S(1)}, bf16[1,33,2048]{2,1,0:T(8,128)(2,1)S(1)}, u32[]{:S(2)}, u32[]{:S(2)}) %collective-permute-start.1) | collective-permute-done | bytes 135200 | tf_op jit(solution)/shard_map/while/body/eval_jaxpr/ppermute | solution.py:12
  402.3 8.5 %conditional.13 = (bf16[1,33,2048]{2,1,0:T(8,128)(2,1)S(1)}, bf16[1,33,2048]{2,1,0:T(8,128)(2,1)S(1)}) conditional(s32[]{:T(128)} %convert_element_type.144, bf16[1,33,2048]{2,1,0:T(8,128)(2,1)S(1)} %get-tuple-element.973, (bf16[1,33,2048]{2,1,0:T(8,128)(2,1)S(1)}, s32[]{:T(128)}, bf16[6,1,33,2048]{3,2,1,0:T(8,128)(2,1)S(1)}, ...), branch_computations={%region_12.12_spmd, %region_13.14_spmd} | conditional | flops 554866688 | bytes 53235792 | solution.py:183
  414.7 13.4 %collective-permute-done.1 = bf16[1,33,2048]{2,1,0:T(8,128)(2,1)S(1)} collective-permute-done((bf16[1,33,2048]{2,1,0:T(8,128)(2,1)S(1)}, bf16[1,33,2048]{2,1,0:T(8,128)(2,1)S(1)}, u32[]{:S(2)}, u32[]{:S(2)}) %collective-permute-start.1) | collective-permute-done | bytes 135200 | tf_op jit(solution)/shard_map/while/body/eval_jaxpr/ppermute | solution.py:12
  428.7 8.5 %conditional.13 = (bf16[1,33,2048]{2,1,0:T(8,128)(2,1)S(1)}, bf16[1,33,2048]{2,1,0:T(8,128)(2,1)S(1)}) conditional(s32[]{:T(128)} %convert_element_type.144, bf16[1,33,2048]{2,1,0:T(8,128)(2,1)S(1)} %get-tuple-element.973, (bf16[1,33,2048]{2,1,0:T(8,128)(2,1)S(1)}, s32[]{:T(128)}, bf16[6,1,33,2048]{3,2,1,0:T(8,128)(2,1)S(1)}, ...), branch_computations={%region_12.12_spmd, %region_13.14_spmd} | conditional | flops 554866688 | bytes 53235792 | solution.py:183
  441.1 13.4 %collective-permute-done.1 = bf16[1,33,2048]{2,1,0:T(8,128)(2,1)S(1)} collective-permute-done((bf16[1,33,2048]{2,1,0:T(8,128)(2,1)S(1)}, bf16[1,33,2048]{2,1,0:T(8,128)(2,1)S(1)}, u32[]{:S(2)}, u32[]{:S(2)}) %collective-permute-start.1) | collective-permute-done | bytes 135200 | tf_op jit(solution)/shard_map/while/body/eval_jaxpr/ppermute | solution.py:12
  455.1 8.5 %conditional.13 = (bf16[1,33,2048]{2,1,0:T(8,128)(2,1)S(1)}, bf16[1,33,2048]{2,1,0:T(8,128)(2,1)S(1)}) conditional(s32[]{:T(128)} %convert_element_type.144, bf16[1,33,2048]{2,1,0:T(8,128)(2,1)S(1)} %get-tuple-element.973, (bf16[1,33,2048]{2,1,0:T(8,128)(2,1)S(1)}, s32[]{:T(128)}, bf16[6,1,33,2048]{3,2,1,0:T(8,128)(2,1)S(1)}, ...), branch_computations={%region_12.12_spmd, %region_13.14_spmd} | conditional | flops 554866688 | bytes 53235792 | solution.py:183
  467.5 13.4 %collective-permute-done.1 = bf16[1,33,2048]{2,1,0:T(8,128)(2,1)S(1)} collective-permute-done((bf16[1,33,2048]{2,1,0:T(8,128)(2,1)S(1)}, bf16[1,33,2048]{2,1,0:T(8,128)(2,1)S(1)}, u32[]{:S(2)}, u32[]{:S(2)}) %collective-permute-start.1) | collective-permute-done | bytes 135200 | tf_op jit(solution)/shard_map/while/body/eval_jaxpr/ppermute | solution.py:12
  481.6 8.5 %conditional.13 = (bf16[1,33,2048]{2,1,0:T(8,128)(2,1)S(1)}, bf16[1,33,2048]{2,1,0:T(8,128)(2,1)S(1)}) conditional(s32[]{:T(128)} %convert_element_type.144, bf16[1,33,2048]{2,1,0:T(8,128)(2,1)S(1)} %get-tuple-element.973, (bf16[1,33,2048]{2,1,0:T(8,128)(2,1)S(1)}, s32[]{:T(128)}, bf16[6,1,33,2048]{3,2,1,0:T(8,128)(2,1)S(1)}, ...), branch_computations={%region_12.12_spmd, %region_13.14_spmd} | conditional | flops 554866688 | bytes 53235792 | solution.py:183
  493.9 13.4 %collective-permute-done.1 = bf16[1,33,2048]{2,1,0:T(8,128)(2,1)S(1)} collective-permute-done((bf16[1,33,2048]{2,1,0:T(8,128)(2,1)S(1)}, bf16[1,33,2048]{2,1,0:T(8,128)(2,1)S(1)}, u32[]{:S(2)}, u32[]{:S(2)}) %collective-permute-start.1) | collective-permute-done | bytes 135200 | tf_op jit(solution)/shard_map/while/body/eval_jaxpr/ppermute | solution.py:12
  508.0 8.5 %conditional.13 = (bf16[1,33,2048]{2,1,0:T(8,128)(2,1)S(1)}, bf16[1,33,2048]{2,1,0:T(8,128)(2,1)S(1)}) conditional(s32[]{:T(128)} %convert_element_type.144, bf16[1,33,2048]{2,1,0:T(8,128)(2,1)S(1)} %get-tuple-element.973, (bf16[1,33,2048]{2,1,0:T(8,128)(2,1)S(1)}, s32[]{:T(128)}, bf16[6,1,33,2048]{3,2,1,0:T(8,128)(2,1)S(1)}, ...), branch_computations={%region_12.12_spmd, %region_13.14_spmd} | conditional | flops 554866688 | bytes 53235792 | solution.py:183
  522.5 6.8 %bitcast_convert_fusion = bf16[2048,2048]{1,0:T(8,128)(2,1)} fusion(bf16[6,1,33,2048]{3,2,1,0:T(8,128)(2,1)} %get-tuple-element.662, bf16[6,1,33,2048]{3,2,1,0:T(8,128)(2,1)S(1)} %get-tuple-element.1109), kind=kOutput, calls=%fused_computation.68 | convolution fusion | flops 1665138688 | bytes 10010624 | tf_op jit(solution)/shard_map/dot_general | solution.py:203
  530.0 25.8 %all-to-all-start.2 = ((f32[32,1,1]{2,1,0:T(1,128)}), f32[32,1,1]{2,1,0:T(1,128)S(1)}, u32[]{:S(2)}, u32[]{:S(2)}) async-start(f32[32,1,1]{2,1,0:T(1,128)} %broadcast_in_dim.76), calls=%async_computation.3 | async-start | bytes 32768 | tf_op jit(solution)/shard_map/all_to_all | solution.py:28
  568.6 70.3 %all-to-all-done = bf16[32,64,1024]{2,1,0:T(8,128)(2,1)} async-done(((bf16[32,64,1024]{2,1,0:T(8,128)(2,1)}), bf16[32,64,1024]{2,1,0:T(8,128)(2,1)}, u32[]{:S(2)}, u32[]{:S(2)}) %all-to-all-start) | async-done | bytes 4194336 | tf_op jit(solution)/shard_map/all_to_all | solution.py:22
  (401 shorter events, 404.1 us)
Async XLA Ops:
  7.2 82.7 %all-gather.3.cloned.1.call-start = ((), (), s32[]{:S(2)}) async-start(), calls=%async_computation.6 | async-start | bytes 8912896 | tf_op jit(solution)/shard_map/all_gather | solution.py:83
  7.9 654.4 %reduce-scatter.2.cloned.1.call-start = ((), (), s32[]{:S(2)}) async-start(), calls=%async_computation.5 | async-start | bytes 8650752 | tf_op jit(solution)/shard_map/reduce_scatter | solution.py:202
  102.0 4.3 collective-permute-start
  118.2 3.5 collective-permute-start
  133.6 3.5 collective-permute-start
  149.0 3.5 collective-permute-start
  190.2 4.4 collective-permute-start
  258.6 6.5 collective-permute-start.1
  265.8 6.4 collective-permute-start.1
  272.8 6.1 collective-permute-start.1
  279.6 6.1 collective-permute-start.1
  286.3 6.1 collective-permute-start.1
  293.1 7.0 %collective-permute-start.1 = (bf16[1,33,2048]{2,1,0:T(8,128)(2,1)S(1)}, bf16[1,33,2048]{2,1,0:T(8,128)(2,1)S(1)}, u32[]{:S(2)}, u32[]{:S(2)}) collective-permute-start(bf16[1,33,2048]{2,1,0:T(8,128)(2,1)S(1)} %get-tuple-element.974), channel_id=1, source_target_pairs={{16,0},{32,16},{48,32},{64,48},{80,64},{96,80},{112,96},{17,1},{33... | collective-permute-start | bytes 405512 | tf_op jit(solution)/shard_map/while/body/eval_jaxpr/ppermute | solution.py:12
  300.8 74.5 %collective-permute-start.1 = (bf16[1,33,2048]{2,1,0:T(8,128)(2,1)S(1)}, bf16[1,33,2048]{2,1,0:T(8,128)(2,1)S(1)}, u32[]{:S(2)}, u32[]{:S(2)}) collective-permute-start(bf16[1,33,2048]{2,1,0:T(8,128)(2,1)S(1)} %get-tuple-element.974), channel_id=1, source_target_pairs={{16,0},{32,16},{48,32},{64,48},{80,64},{96,80},{112,96},{17,1},{33... | collective-permute-start | bytes 405512 | tf_op jit(solution)/shard_map/while/body/eval_jaxpr/ppermute | solution.py:12
  384.4 17.3 %collective-permute-start.1 = (bf16[1,33,2048]{2,1,0:T(8,128)(2,1)S(1)}, bf16[1,33,2048]{2,1,0:T(8,128)(2,1)S(1)}, u32[]{:S(2)}, u32[]{:S(2)}) collective-permute-start(bf16[1,33,2048]{2,1,0:T(8,128)(2,1)S(1)} %get-tuple-element.974), channel_id=1, source_target_pairs={{16,0},{32,16},{48,32},{64,48},{80,64},{96,80},{112,96},{17,1},{33... | collective-permute-start | bytes 405512 | tf_op jit(solution)/shard_map/while/body/eval_jaxpr/ppermute | solution.py:12
  410.8 17.3 %collective-permute-start.1 = (bf16[1,33,2048]{2,1,0:T(8,128)(2,1)S(1)}, bf16[1,33,2048]{2,1,0:T(8,128)(2,1)S(1)}, u32[]{:S(2)}, u32[]{:S(2)}) collective-permute-start(bf16[1,33,2048]{2,1,0:T(8,128)(2,1)S(1)} %get-tuple-element.974), channel_id=1, source_target_pairs={{16,0},{32,16},{48,32},{64,48},{80,64},{96,80},{112,96},{17,1},{33... | collective-permute-start | bytes 405512 | tf_op jit(solution)/shard_map/while/body/eval_jaxpr/ppermute | solution.py:12
  437.2 17.3 %collective-permute-start.1 = (bf16[1,33,2048]{2,1,0:T(8,128)(2,1)S(1)}, bf16[1,33,2048]{2,1,0:T(8,128)(2,1)S(1)}, u32[]{:S(2)}, u32[]{:S(2)}) collective-permute-start(bf16[1,33,2048]{2,1,0:T(8,128)(2,1)S(1)} %get-tuple-element.974), channel_id=1, source_target_pairs={{16,0},{32,16},{48,32},{64,48},{80,64},{96,80},{112,96},{17,1},{33... | collective-permute-start | bytes 405512 | tf_op jit(solution)/shard_map/while/body/eval_jaxpr/ppermute | solution.py:12
  463.6 17.3 %collective-permute-start.1 = (bf16[1,33,2048]{2,1,0:T(8,128)(2,1)S(1)}, bf16[1,33,2048]{2,1,0:T(8,128)(2,1)S(1)}, u32[]{:S(2)}, u32[]{:S(2)}) collective-permute-start(bf16[1,33,2048]{2,1,0:T(8,128)(2,1)S(1)} %get-tuple-element.974), channel_id=1, source_target_pairs={{16,0},{32,16},{48,32},{64,48},{80,64},{96,80},{112,96},{17,1},{33... | collective-permute-start | bytes 405512 | tf_op jit(solution)/shard_map/while/body/eval_jaxpr/ppermute | solution.py:12
  490.0 17.3 %collective-permute-start.1 = (bf16[1,33,2048]{2,1,0:T(8,128)(2,1)S(1)}, bf16[1,33,2048]{2,1,0:T(8,128)(2,1)S(1)}, u32[]{:S(2)}, u32[]{:S(2)}) collective-permute-start(bf16[1,33,2048]{2,1,0:T(8,128)(2,1)S(1)} %get-tuple-element.974), channel_id=1, source_target_pairs={{16,0},{32,16},{48,32},{64,48},{80,64},{96,80},{112,96},{17,1},{33... | collective-permute-start | bytes 405512 | tf_op jit(solution)/shard_map/while/body/eval_jaxpr/ppermute | solution.py:12
  516.5 6.1 collective-permute-start.1
  530.0 32.7 %all-to-all-start.2 = ((f32[32,1,1]{2,1,0:T(1,128)}), f32[32,1,1]{2,1,0:T(1,128)S(1)}, u32[]{:S(2)}, u32[]{:S(2)}) async-start(f32[32,1,1]{2,1,0:T(1,128)} %broadcast_in_dim.76), calls=%async_computation.3 | async-start | bytes 32768 | tf_op jit(solution)/shard_map/all_to_all | solution.py:28
  562.6 76.2 %all-to-all-start = ((bf16[32,64,1024]{2,1,0:T(8,128)(2,1)}), bf16[32,64,1024]{2,1,0:T(8,128)(2,1)}, u32[]{:S(2)}, u32[]{:S(2)}) async-start(bf16[32,64,1024]{2,1,0:T(8,128)(2,1)} %bitcast.121), calls=%async_computation.1 | async-start | bytes 8388608 | tf_op jit(solution)/shard_map/all_to_all | solution.py:22
  640.1 9.7 %all-to-all-start.3 = ((bf16[8,1,1]{2,1,0:T(2,128)(2,1)}), bf16[8,1,1]{2,1,0:T(2,128)(2,1)S(1)}, u32[]{:S(2)}, u32[]{:S(2)}) async-start(bf16[8,1,1]{2,1,0:T(2,128)(2,1)} %transpose_reshape.3), calls=%async_computation.4 | async-start | bytes 8192 | tf_op jit(solution)/shard_map/all_to_all | solution.py:22
  649.8 11.8 %all-to-all-start.1 = ((bf16[8,64,128]{2,1,0:T(8,128)(2,1)}), bf16[8,64,128]{2,1,0:T(8,128)(2,1)S(1)}, u32[]{:S(2)}, u32[]{:S(2)}) async-start(bf16[8,64,128]{2,1,0:T(8,128)(2,1)} %copy.31), calls=%async_computation.2 | async-start | bytes 262144 | tf_op jit(solution)/shard_map/all_to_all | solution.py:22
  (14 other events, 63.0 us)
Sparse Core Ops, SparseCore 0:
  10.4 79.4 all-gather.2
  529.5 125.3 reduce-scatter.1
where the time goes:
time: 676 us; the launch traced here: 672 us
  waiting for transfers between devices  318 us (47%)
  matrix products  109 us (16%)
  starting transfers between devices  73.1 us (11%)
  local copies, waits for them, and re-layouts  67.7 us (10%)
  blocking collectives  34.4 us (5%)
  other arithmetic  27 us (4%)
  loops' own time  26.6 us (4%)
  between operations  15.9 us (2%)
    ppermute x26, waiting for transfers between devices, from_behind(): lax.ppermute(value, axis, [(source, source + steps) for source in range(i...  188 us
    all_to_all x3, waiting for transfers between devices, sent_and_summed(): lax.all_to_all(parts, axis, split_axis=0, concat_axis=0, tiled=True)  79.3 us
    all_gather x1, waiting for transfers between devices, local(): layer_full = lax.all_gather(layers[0], 'mp', axis=0, tiled=True)  45.4 us
    ppermute x26, starting transfers between devices, from_behind(): lax.ppermute(value, axis, [(source, source + steps) for source in range(i...  34.6 us
    psum x1, blocking collectives, local(): lax.psum(jnp.sum(sample_total[sample_order].reshape(MB, per_batch), axis=...  34.4 us
    dot_general x6, matrix products, backward_active(): jnp.dot(row_block.reshape(-1, model_width), layer_full, preferred_element...  30.4 us
    dot_general x6, matrix products, forward_layer(): jnp.dot(row_block.reshape(-1, model_width), weight, preferred_element_typ...  29.5 us
    dot_general x13, matrix products, lift_batch(): jnp.dot(rows_in.reshape(-1, in_width), encoder, preferred_element_type=jn...  26.7 us
  transfers between devices with their start and end apart: 32, of which 31 were waited for; matrix products, arithmetic and copies ran while one was open for 6% of the time, Pallas kernels for 0%

commit v1 on v0

v1 whole, which is shorter than its diff:
```python
import functools

import jax
import jax.numpy as jnp
from jax import lax
from jax.experimental import pallas as pl
from jax.experimental.pallas import tpu as pltpu
from jax.sharding import PartitionSpec as P

MB = 6
ROWS = 48
MESH = pl.DeviceIdType.MESH


def first_row(row, height):
    rows = lax.broadcasted_iota(jnp.int32, (height, row.shape[1]), 0)
    return jnp.where(rows == 0, jnp.broadcast_to(row, (height, row.shape[1])), 0.0)


def relay_kernel(
    sections, pieces,
    h0, h0p, w, head, head_t, want, coef,
    o_in, o_mix, o_out, o_cot, o_loss,
    xin, pin, pout, pre, thb, cin, cpin, cout, cpout,
    fsend, frecv, bsend, brecv,
):
    n_mb, rows, width = xin.shape
    rank = cin.shape[1]
    out_width = head.shape[1]
    tile = width // pieces
    s = lax.axis_index("section")
    nxt = lax.rem(s + 1, sections)
    prv = lax.rem(s + sections - 1, sections)
    first = s == 0
    last = s == sections - 1

    barrier = pltpu.get_barrier_semaphore()
    for other in (nxt, prv):
        pl.semaphore_signal(barrier, inc=1, device_id={"section": other}, device_id_type=MESH)
    pl.semaphore_wait(barrier, 2)

    def fcopy(m, j):
        cols = pl.ds(j * tile, tile)
        return pltpu.make_async_remote_copy(
            src_ref=o_out.at[m, pl.ds(0, rank), cols],
            dst_ref=xin.at[m, pl.ds(0, rank), cols],
            send_sem=fsend.at[m, j], recv_sem=frecv.at[m, j],
            device_id={"section": nxt}, device_id_type=MESH,
        )

    def fpcopy(m):
        return pltpu.make_async_remote_copy(
            src_ref=pout.at[m], dst_ref=pin.at[m],
            send_sem=fsend.at[m, pieces], recv_sem=frecv.at[m, pieces],
            device_id={"section": nxt}, device_id_type=MESH,
        )

    def bcopy(m, j):
        cols = pl.ds(j * tile, tile)
        return pltpu.make_async_remote_copy(
            src_ref=cout.at[m, :, cols], dst_ref=cin.at[m, :, cols],
            send_sem=bsend.at[m, j], recv_sem=brecv.at[m, j],
            device_id={"section": prv}, device_id_type=MESH,
        )

    def bpcopy(m):
        return pltpu.make_async_remote_copy(
            src_ref=cpout.at[m], dst_ref=cpin.at[m],
            send_sem=bsend.at[m, pieces], recv_sem=brecv.at[m, pieces],
            device_id={"section": prv}, device_id_type=MESH,
        )

    @pl.when(first)
    def _():
        xin[...] = h0[...]
        pin[...] = h0p[...]

    def forward(m, _):
        @pl.when(jnp.logical_not(first))
        def _():
            for j in range(pieces):
                fcopy(m, j).wait_recv()
            fpcopy(m).wait_recv()
            xin[m, pl.ds(rank, rows - rank), :] = first_row(pin[m], rows - rank).astype(jnp.bfloat16)

        for j in range(pieces):
            cols = pl.ds(j * tile, tile)
            acc = jnp.dot(xin[m], w[:, cols], preferred_element_type=jnp.float32)
            th = jnp.tanh(acc[rank : rank + 1, :])
            slope = 1.0 - th * th
            tangent = acc[:rank, :]
            pre[m, :, cols] = tangent
            thb[m, :, cols] = th
            moved = xin[m, pl.ds(0, rank), cols].astype(jnp.float32) + slope * tangent
            o_out[m, pl.ds(0, rank), cols] = moved.astype(jnp.bfloat16)
            primal = (pin[m, :, cols] + th).astype(jnp.bfloat16).astype(jnp.float32)
            pout[m, :, cols] = primal
            o_out[m, pl.ds(rank, rows - rank), cols] = first_row(primal, rows - rank).astype(jnp.bfloat16)

            @pl.when(jnp.logical_not(last))
            def _():
                fcopy(m, j).start()

        @pl.when(jnp.logical_not(last))
        def _():
            fpcopy(m).start()

        return 0

    lax.fori_loop(0, n_mb, forward, 0)

    @pl.when(jnp.logical_not(last))
    def _():
        o_cot[...] = jnp.zeros_like(o_cot)
        o_loss[...] = jnp.zeros_like(o_loss)

    @pl.when(last)
    def _():
        step = 256 if out_width % 256 == 0 else out_width
        total = jnp.zeros((1, 1), jnp.float32)
        scale = coef[...]
        for n in range(out_width // step):
            cols = pl.ds(n * step, step)
            outputs = jnp.dot(
                o_out[...].reshape(n_mb * rows, width), head[:, cols],
                preferred_element_type=jnp.float32,
            )
            mismatch = outputs - want[:, cols].astype(jnp.float32)
            weighted = scale * mismatch
            total = total + jnp.sum(
                jnp.sum(weighted * mismatch, axis=0, keepdims=True), axis=1, keepdims=True
            )
            o_cot[:, cols] = (2.0 * weighted).astype(jnp.bfloat16)
        o_loss[...] = jnp.broadcast_to(total, o_loss.shape)
        for n in range(width // step):
            cols = pl.ds(n * step, step)
            grads = jnp.dot(o_cot[...], head_t[:, cols], preferred_element_type=jnp.float32)
            grads = grads.astype(jnp.bfloat16)
            for m in range(n_mb):
                cin[m, :, cols] = grads[m * rows : m * rows + rank, :]
                cpin[m, :, cols] = grads[m * rows + rank : m * rows + rows, :].astype(jnp.float32)[0:1]

    def backward(m, _):
        @pl.when(jnp.logical_not(last))
        def _():
            for j in range(pieces):
                bcopy(m, j).wait_recv()
            bpcopy(m).wait_recv()

        for j in range(pieces):
            cols = pl.ds(j * tile, tile)
            upstream = cin[m, :, cols].astype(jnp.float32)
            th = thb[m, :, cols]
            slope = 1.0 - th * th
            o_mix[m, pl.ds(0, rank), cols] = (upstream * slope).astype(jnp.bfloat16)
            total = jnp.sum(upstream * pre[m, :, cols], axis=0, keepdims=True)
            primal = cpin[m, :, cols] * slope - 2.0 * total * th * slope
            o_mix[m, pl.ds(rank, rows - rank), cols] = first_row(primal, rows - rank).astype(jnp.bfloat16)

        @pl.when(jnp.logical_not(first))
        def _():
            for j in range(pieces):
                cols = pl.ds(j * tile, tile)
                back = lax.dot_general(
                    o_mix[m], w[cols, :], (((1,), (1,)), ((), ())),
                    preferred_element_type=jnp.float32,
                )
                cout[m, :, cols] = (cin[m, :, cols].astype(jnp.float32) + back[:rank]).astype(jnp.bfloat16)
                cpout[m, :, cols] = (
                    (cpin[m, :, cols] + back[rank : rank + 1]).astype(jnp.bfloat16).astype(jnp.float32)
                )
                bcopy(m, j).start()
            bpcopy(m).start()

        return 0

    lax.fori_loop(0, n_mb, backward, 0)
    o_in[...] = xin[...]

    def drain(m, _):
        @pl.when(jnp.logical_not(last))
        def _():
            for j in range(pieces):
                fcopy(m, j).wait_send()
            fpcopy(m).wait_send()

        @pl.when(jnp.logical_not(first))
        def _():
            for j in range(pieces):
                bcopy(m, j).wait_send()
            bpcopy(m).wait_send()

        return 0

    lax.fori_loop(0, n_mb, drain, 0)


def relay(sections, h0, h0p, w, head, head_t, want, coef):
    n_mb, rows, width = h0.shape
    rank = 32
    out_width = head.shape[1]
    pieces = 4
    bf16, f32 = jnp.bfloat16, jnp.float32
    vmem = pl.BlockSpec(memory_space=pltpu.VMEM)
    return pl.pallas_call(
        functools.partial(relay_kernel, sections, pieces),
        out_shape=(
            jax.ShapeDtypeStruct((n_mb, rows, width), bf16),
            jax.ShapeDtypeStruct((n_mb, rows, width), bf16),
            jax.ShapeDtypeStruct((n_mb, rows, width), bf16),
            jax.ShapeDtypeStruct((n_mb * rows, out_width), bf16),
            jax.ShapeDtypeStruct((8, 128), f32),
        ),
        in_specs=[vmem] * 7,
        out_specs=(vmem,) * 5,
        scratch_shapes=[
            pltpu.VMEM((n_mb, rows, width), bf16),
            pltpu.VMEM((n_mb, 1, width), f32),
            pltpu.VMEM((n_mb, 1, width), f32),
            pltpu.VMEM((n_mb, rank, width), f32),
            pltpu.VMEM((n_mb, 1, width), f32),
            pltpu.VMEM((n_mb, rank, width), bf16),
            pltpu.VMEM((n_mb, 1, width), f32),
            pltpu.VMEM((n_mb, rank, width), bf16),
            pltpu.VMEM((n_mb, 1, width), f32),
            pltpu.SemaphoreType.DMA((n_mb, pieces + 1)),
            pltpu.SemaphoreType.DMA((n_mb, pieces + 1)),
            pltpu.SemaphoreType.DMA((n_mb, pieces + 1)),
            pltpu.SemaphoreType.DMA((n_mb, pieces + 1)),
        ],
        compiler_params=pltpu.CompilerParams(
            collective_id=0, has_side_effects=True, vmem_limit_bytes=60 * 1024 * 1024
        ),
        name="relay",
    )(h0, h0p, w, head, head_t, want, coef)


def sample_rows(primal, tangents):
    count, rank, width = tangents.shape
    zeros = jnp.zeros((count, ROWS - rank - 1, width), tangents.dtype)
    return jnp.concatenate([tangents, primal[:, None], zeros], axis=1)


def local(
    inputs, tangents, targets, target_jac, rank_mask, batch_order, encoder, layers, head_weight
):
    samples, rank, in_width = tangents.shape
    width = layers.shape[2]
    out_width = head_weight.shape[1]
    sections = lax.axis_size("section")
    f32 = jnp.float32
    weight = lax.all_gather(layers[0], "mp", axis=0, tiled=True)

    mask = rank_mask.astype(f32)
    totals = 1.0 + jnp.sum(mask, axis=1)
    here = (batch_order[0][:, None] == jnp.arange(samples)[None, :]).astype(f32)
    counts = lax.psum(jnp.sum(here * totals[None, :], axis=1), "mp")
    count_of = jnp.sum(here * counts[:, None], axis=0)
    row_weight = jnp.concatenate(
        [mask, jnp.ones((samples, 1), f32), jnp.zeros((samples, ROWS - rank - 1), f32)], axis=1
    )
    coef = (row_weight / count_of[:, None]).reshape(samples * ROWS, 1)

    rows_in = sample_rows(inputs, tangents).reshape(samples * ROWS, in_width)
    lifted = jnp.dot(rows_in, encoder, preferred_element_type=f32).astype(jnp.bfloat16)
    h0 = lifted.reshape(samples, ROWS, width)
    h0p = h0[:, rank : rank + 1].astype(f32)
    want = sample_rows(targets, target_jac).reshape(samples * ROWS, out_width)

    x_in, mix, x_out, cot, loss = relay(
        sections, h0, h0p, weight, head_weight, head_weight.T, want, coef
    )
    flat = lambda a: a.reshape(samples * ROWS, -1)
    grad_layer = jnp.dot(flat(x_in).T, flat(mix), preferred_element_type=f32)
    grad_head = jnp.dot(flat(x_out).T, cot, preferred_element_type=f32)
    both = jnp.concatenate([grad_layer.astype(jnp.bfloat16), grad_head.astype(jnp.bfloat16)], axis=1)
    summed = lax.psum_scatter(both, ("dp", "mp"), scatter_dimension=0, tiled=True)
    grad_layers = summed[:, :width].astype(f32)[None]
    parts = jnp.moveaxis(summed[:, width:].reshape(summed.shape[0], sections, -1), 1, 0)
    arrived = lax.all_to_all(parts, "section", split_axis=0, concat_axis=0, tiled=True)
    grad_head_out = arrived[sections - 1].astype(f32)
    loss_sum = lax.psum(loss[0, 0], ("dp", "section", "mp"))
    loss_value = loss_sum / (lax.axis_size("dp") * MB * out_width)
    return grad_layers, grad_head_out, loss_value


def solution(mesh):
    in_specs = (
        P(("dp", "mp"), None),
        P(("dp", "mp"), None, None),
        P(("dp", "mp"), None),
        P(("dp", "mp"), None, None),
        P(("dp", "mp"), None),
        P(("dp", "mp"), None),
        P(),
        P("section", "mp", None),
        P(),
    )
    out_specs = (P("section", ("dp", "mp"), None), P(("dp", "mp"), "section"), P())
    return jax.shard_map(local, mesh=mesh, in_specs=in_specs, out_specs=out_specs, check_vma=False)
```

time: 676 us -> 396 us (0.59)
  waiting for transfers between devices: 318 us -> 66.1 us
  Pallas kernels: 0 us -> 126 us
  matrix products: 109 us -> 9.57 us
  blocking collectives: 34.4 us -> 115 us
  starting transfers between devices: 73.1 us -> 6.79 us
  local copies, waits for them, and re-layouts: 67.7 us -> 32.1 us
  loops' own time: 26.6 us -> 0 us
    ppermute x26 -> x0, waiting for transfers between devices: 188 us -> none  [from_behind(): lax.ppermute(value, axis, [(source, source + steps) for source in range(i...]
    pallas_call x0 -> x1, Pallas kernels: none -> 126 us  [relay(): pl.pallas_call(functools.partial(relay_kernel, sections, pieces), out_sha...]
    dot_general x32 -> x3, matrix products: 109 us -> 9.57 us  [the longest x1 4.81 us: local(): grad_layer = jnp.dot(flat(x_in).T, flat(mix), preferred_element_type=f32)]
    psum x1 -> x2, blocking collectives: 34.4 us -> 115 us  [the longest x1 80.3 us: local(): loss_sum = lax.psum(loss[0, 0], ('dp', 'section', 'mp'))]
    all_to_all x4 -> x1, waiting for transfers between devices: 83.6 us -> 3.57 us  [local(): lax.all_to_all(parts, 'section', split_axis=0, concat_axis=0, tiled=True)]
    ppermute x26 -> x0, starting transfers between devices: 34.6 us -> none  [from_behind(): lax.ppermute(value, axis, [(source, source + steps) for source in range(i...]
    all_to_all x4 -> x1, starting transfers between devices: 38.5 us -> 6.72 us  [local(): lax.all_to_all(parts, 'section', split_axis=0, concat_axis=0, tiled=True)]
    dynamic_slice x65 -> x0, local copies, waits for them, and re-layouts: 29.8 us -> none  [the longest x13 17 us: picked_of(): lax.dynamic_slice_in_dim(sample_order, batch_slot * per_batch, per_batch)]
  transfers between devices with their start and end apart: 32 -> 3, of which waited for: 31 -> 3; matrix products, arithmetic and copies ran while one was open for 6% -> 5% of each run, Pallas kernels for 0% -> 0%
where the time goes in v1:
time: 396 us; the launch traced here: 392 us
  Pallas kernels  126 us (32%)
  blocking collectives  115 us (29%)
  waiting for transfers between devices  66.1 us (17%)
  local copies, waits for them, and re-layouts  32.1 us (8%)
  other arithmetic  21.1 us (5%)
  between operations  16 us (4%)
  matrix products  9.57 us (2%)
  starting transfers between devices  6.79 us (2%)
    pallas_call x1, Pallas kernels, relay(): pl.pallas_call(functools.partial(relay_kernel, sections, pieces), out_sha...  126 us
    psum x1, blocking collectives, local(): loss_sum = lax.psum(loss[0, 0], ('dp', 'section', 'mp'))  80.3 us
    psum x1, blocking collectives, local(): counts = lax.psum(jnp.sum(here * totals[None, :], axis=1), 'mp')  34.5 us
    all_gather x1, waiting for transfers between devices, local(): weight = lax.all_gather(layers[0], 'mp', axis=0, tiled=True)  32.4 us
    unnamed x3, waiting for transfers between devices  30.1 us
    unnamed x19, local copies, waits for them, and re-layouts  25.6 us
    concatenate x1, other arithmetic, local(): jnp.concatenate([grad_layer.astype(jnp.bfloat16), grad_head.astype(jnp.bf...  14.4 us
  transfers between devices with their start and end apart: 3, of which 3 were waited for; matrix products, arithmetic and copies ran while one was open for 5% of the time, Pallas kernels for 0%

profile of v1, /device:TPU:1, one launch (start us, length us, event | category | flops | bytes accessed | tf_op | source)
XLA Modules:
  0.0 392.5 jit_solution(17416835229581447147)
XLA Ops:
  8.0 0.8 convert_reduce_fusion
  8.8 0.8 select_reduce_fusion.1
  9.6 34.5 %psum.14 = f32[6]{0:T(128)S(1)} all-reduce(f32[6]{0:T(128)S(1)} %select_reduce_fusion.1), channel_id=1, replica_groups=mesh['dp'=2,'section'=8,'mp'=16] {'mp'}, use_global_device_ids=true, to_apply=%region_2.0 | all-reduce | flops 6 | bytes 48 | tf_op jit(solution)/shard_map/psum | solution.py:257
  47.3 0.8 div.25.coef
  48.1 6.7 %copy.28 = bf16[2048,1024]{0,1:T(8,128)(2,1)} copy(bf16[2048,1024]{1,0:T(8,128)(2,1)} %head.1) | data formatting | bytes 8388608 | tf_op args[8]
  55.0 1.0 maximum_maximum_fusion
  55.9 0.8 convolution_convert_fusion.1
  57.5 32.4 %all-gather.3.cloned.1.call-done = bf16[1,2048,2048]{2,1,0:T(8,128)(2,1)} async-done(((bf16[1,128,2048]{2,1,0:T(8,128)(2,1)}), bf16[1,2048,2048]{2,1,0:T(8,128)(2,1)}) %all-gather.3.cloned.1.call-update) | async-done | bytes 8388624 | tf_op jit(solution)/shard_map/all_gather | solution.py:252
  89.9 126.0 %relay.1 = (bf16[6,48,2048]{2,1,0:T(8,128)(2,1)}, bf16[6,48,2048]{2,1,0:T(8,128)(2,1)}, bf16[6,48,2048]{2,1,0:T(8,128)(2,1)}, bf16[288,1024]{1,0:T(8,128)(2,1)}, f32[8,128]{1,0:T(8,128)}) custom-call(bf16[6,48,2048]{2,1,0:T(8,128)(2,1)} %bitcast.34, f32[6,1,2048]{2,1,0:T(1,128)} %slice_convert_fusion.h0p, bf16[2048,2048]{1,0:T(8,128)(2,1)} %bitcast.31, ...), custom_call_target="tpu_custom_call" | custom-call | tf_op jit(solution)/shard_map/relay/pallas_call | solution.py:205
  215.9 4.0 %convolution_convert_fusion = bf16[2048,1024]{0,1:T(8,128)(2,1)S(1)} fusion(bf16[288,2048]{1,0:T(8,128)(2,1)} %bitcast.39, bf16[288,1024]{1,0:T(8,128)(2,1)} %get-tuple-element.11), kind=kOutput, calls=%fused_computation.2 | convolution fusion | flops 1210056704 | bytes 5963776 | tf_op jit(solution)/shard_map/dot_general | solution.py:275
  219.9 4.8 %bitcast_convert_fusion = bf16[2048,2048]{0,1:T(8,128)(2,1)S(1)} fusion(bf16[6,48,2048]{2,1,0:T(8,128)(2,1)S(1)} %copy-done.5, bf16[6,48,2048]{2,1,0:T(8,128)(2,1)S(1)} %copy-done.6), kind=kOutput, calls=%fused_computation | convolution fusion | flops 2420113408 | bytes 10747904 | tf_op jit(solution)/shard_map/dot_general | solution.py:274
  224.7 14.4 %pad_maximum_fusion = bf16[2048,3072]{0,1:T(8,128)(2,1)} fusion(bf16[2048,1024]{0,1:T(8,128)(2,1)S(1)} %convolution_convert_fusion, bf16[2048,2048]{0,1:T(8,128)(2,1)S(1)} %bitcast_convert_fusion), kind=kLoop, calls=%fused_computation.1 | loop fusion | flops 25165824 | bytes 25165824 | tf_op jit(solution)/shard_map/concatenate | solution.py:276
  239.2 16.6 %copy.33 = bf16[2048,3072]{1,0:T(8,128)(2,1)} copy(bf16[2048,3072]{0,1:T(8,128)(2,1)} %pad_maximum_fusion) | data formatting | bytes 25165824
  255.8 1.2 slice.19
  257.0 80.3 %psum.15 = f32[]{:T(128)} all-reduce(f32[]{:T(128)} %bitcast.14), channel_id=1, replica_groups=mesh['dp'=2,'section'=8,'mp'=16] {'dp','section','mp'}, use_global_device_ids=true, to_apply=%region_5.0 | all-reduce | flops 1 | bytes 8 | tf_op jit(solution)/shard_map/psum | solution.py:282
  338.0 29.4 %reduce-scatter.4.cloned.1.call-done = bf16[64,3072]{1,0:T(8,128)(2,1)} async-done(((bf16[2048,3072]{1,0:T(8,128)(2,1)}), bf16[64,3072]{1,0:T(8,128)(2,1)}) %reduce-scatter.4.cloned.1.call-update) | async-done | bytes 393232
  367.4 0.9 slice.22
  368.5 0.8 copy.31
  369.3 6.7 %all-to-all-start = ((bf16[8,64,128]{2,1,0:T(8,128)(2,1)}), bf16[8,64,128]{2,1,0:T(8,128)(2,1)S(1)}, u32[]{:S(2)}, u32[]{:S(2)}) async-start(bf16[8,64,128]{2,1,0:T(8,128)(2,1)} %bitcast.12), calls=%async_computation | async-start | bytes 262144 | tf_op jit(solution)/shard_map/all_to_all | solution.py:280
  376.0 1.1 slice.21
  377.1 1.0 copy.35
  378.1 1.1 bitcast_convert_fusion.1
  379.2 1.1 copy.32
  380.3 3.6 all-to-all-done
  (33 shorter events, 5.6 us)
Async XLA Ops:
  7.2 48.8 %copy-start = (bf16[512,2048]{1,0:T(8,128)(2,1)S(1)}, bf16[512,2048]{1,0:T(8,128)(2,1)}, u32[]{:S(2)}) copy-start(bf16[512,2048]{1,0:T(8,128)(2,1)} %param.15) | copy-start | bytes 6291460
  7.2 82.7 %all-gather.3.cloned.1.call-start = ((), (), s32[]{:S(2)}) async-start(), calls=%async_computation.2 | async-start | bytes 8912896 | tf_op jit(solution)/shard_map/all_gather | solution.py:252
  7.9 359.5 %reduce-scatter.4.cloned.1.call-start = ((), (), s32[]{:S(2)}) async-start(), calls=%async_computation.3 | async-start | bytes 12976128
  48.1 6.8 %copy-start.4 = (bf16[6,32,512]{2,1,0:T(8,128)(2,1)S(1)}, bf16[6,32,512]{2,1,0:T(8,128)(2,1)}, u32[]{:S(2)}) copy-start(bf16[6,32,512]{2,1,0:T(8,128)(2,1)} %param.10) | copy-start | bytes 589828
  48.1 6.9 %copy-start.3 = (bf16[6,32,1024]{2,1,0:T(8,128)(2,1)S(1)}, bf16[6,32,1024]{2,1,0:T(8,128)(2,1)}, u32[]{:S(2)}) copy-start(bf16[6,32,1024]{2,1,0:T(8,128)(2,1)} %param.12) | copy-start | bytes 1179652
  56.7 33.2 %copy-start.2 = (bf16[288,2048]{1,0:T(8,128)(2,1)}, bf16[288,2048]{1,0:T(8,128)(2,1)S(1)}, u32[]{:S(2)}) copy-start(bf16[288,2048]{1,0:T(8,128)(2,1)S(1)} %convolution_convert_fusion.1) | copy-start | bytes 3538948
  215.9 4.0 %copy-start.5 = (bf16[6,48,2048]{2,1,0:T(8,128)(2,1)S(1)}, bf16[6,48,2048]{2,1,0:T(8,128)(2,1)}, u32[]{:S(2)}) copy-start(bf16[6,48,2048]{2,1,0:T(8,128)(2,1)} %get-tuple-element.8) | copy-start | bytes 3538948
  215.9 4.0 %copy-start.6 = (bf16[6,48,2048]{2,1,0:T(8,128)(2,1)S(1)}, bf16[6,48,2048]{2,1,0:T(8,128)(2,1)}, u32[]{:S(2)}) copy-start(bf16[6,48,2048]{2,1,0:T(8,128)(2,1)} %get-tuple-element.9) | copy-start | bytes 3538948
  369.3 14.6 %all-to-all-start = ((bf16[8,64,128]{2,1,0:T(8,128)(2,1)}), bf16[8,64,128]{2,1,0:T(8,128)(2,1)S(1)}, u32[]{:S(2)}, u32[]{:S(2)}) async-start(bf16[8,64,128]{2,1,0:T(8,128)(2,1)} %bitcast.12), calls=%async_computation | async-start | bytes 262144 | tf_op jit(solution)/shard_map/all_to_all | solution.py:280
  376.0 8.6 %copy-start.1 = (bf16[512,2048]{1,0:T(8,128)(2,1)S(1)}, bf16[512,2048]{1,0:T(8,128)(2,1)}, u32[]{:S(2)}) copy-start(bf16[512,2048]{1,0:T(8,128)(2,1)} %param.15) | copy-start | bytes 6291460
Sparse Core Ops, SparseCore 0:
  10.4 79.4 all-gather.2
  255.9 111.4 reduce-scatter.3

commit v2 on v1

v2 whole, which is shorter than its diff:
```python
import functools

import jax
import jax.numpy as jnp
from jax import lax
from jax.experimental import pallas as pl
from jax.experimental.pallas import tpu as pltpu
from jax.sharding import PartitionSpec as P

SIDE = 4
ROWS = 48
PIECES = 4
MESH = pl.DeviceIdType.MESH
BF16, F32 = jnp.bfloat16, jnp.float32


def first_row(row, height):
    rows = lax.broadcasted_iota(jnp.int32, (height, row.shape[1]), 0)
    return jnp.where(rows == 0, jnp.broadcast_to(row, (height, row.shape[1])), 0.0)


def stacked_rows(get_row, count, height, width):
    rows = lax.broadcasted_iota(jnp.int32, (height, width), 0)
    block = jnp.zeros((height, width), F32)
    for m in range(count):
        block = jnp.where(rows == m, jnp.broadcast_to(get_row(m), (height, width)), block)
    return block


class Place:
    def __init__(self, sections):
        self.sections = sections
        self.core = lax.axis_index("dp")
        self.s = lax.axis_index("section")
        self.mp = lax.axis_index("mp")
        self.y = self.mp // SIDE
        self.x = lax.rem(self.mp, SIDE)
        self.first = self.s == 0
        self.last = self.s == sections - 1
        self.nxt = lax.rem(self.s + 1, sections)
        self.prv = lax.rem(self.s + sections - 1, sections)

    def along(self, coordinate, steps):
        return lax.rem(coordinate + steps + SIDE, SIDE)

    def chip(self, axis, steps):
        if axis == 0:
            return self.y * SIDE + self.along(self.x, steps)
        return self.along(self.y, steps) * SIDE + self.x


def remote(src, dst, send, recv, device_id):
    return pltpu.make_async_remote_copy(
        src_ref=src, dst_ref=dst, send_sem=send, recv_sem=recv,
        device_id=device_id, device_id_type=MESH,
    )


def enter(place):
    barrier = pltpu.get_barrier_semaphore()
    plane = 2 * SIDE * SIDE
    me = place.core * (SIDE * SIDE) + place.mp

    def tell_plane(step, _):
        other = lax.rem(me + step, plane)
        pl.semaphore_signal(
            barrier, inc=1,
            device_id={"dp": other // (SIDE * SIDE), "mp": lax.rem(other, SIDE * SIDE)},
            device_id_type=MESH,
        )
        return 0

    def tell_column(step, _):
        other = lax.rem(place.s + step, place.sections)
        pl.semaphore_signal(barrier, inc=1, device_id={"section": other}, device_id_type=MESH)
        return 0

    lax.fori_loop(1, plane, tell_plane, 0)
    lax.fori_loop(1, place.sections, tell_column, 0)
    pl.semaphore_wait(barrier, plane - 1 + place.sections - 1)


class Gather:
    def __init__(self, place, shard, w, sems):
        self.p, self.shard, self.w = place, shard, w
        self.send1, self.recv1, self.send2, self.recv2 = sems[:4]
        self.dsend1, self.drecv1, self.dsend2, self.drecv2 = sems[4:]
        self.depth = shard.shape[0]
        self.piece = self.depth // 4

    def rows(self, q, core, step1, step2, half):
        p = self.p
        dx, dy = (step1, step2) if q == 0 else (step2, step1)
        chip = p.along(p.y, dy) * SIDE + p.along(p.x, dx)
        start = chip * self.depth + core * (2 * self.piece) + q * self.piece
        length = self.piece
        if half is not None:
            length = self.piece // 2
            start = start + half * length
        return pl.ds(pl.multiple_of(start, length), length)

    def copy(self, q, phase, o, e):
        p = self.p
        axis = q if phase == 1 else 1 - q
        to = 1 if e in (0, 2) else -1
        back = {0: 0, 1: 0, 2: -1, 3: 1}[e]
        half = {0: None, 1: None, 2: 0, 3: 1}[e]
        step1, step2 = (back, 0) if phase == 1 else (o, back)
        dst = self.w.at[self.rows(q, p.core, step1, step2, half)]
        src = dst
        if step1 == 0 and step2 == 0:
            src = self.shard.at[pl.ds(pl.multiple_of(p.core * (2 * self.piece) + q * self.piece, self.piece), self.piece)]
        send, recv = self.sems(phase, q, o, e, self.send1, self.recv1, self.send2, self.recv2)
        return remote(src, dst, send, recv, {"mp": p.chip(axis, to)})

    def sems(self, phase, q, o, e, send1, recv1, send2, recv2):
        if phase == 1:
            return send1.at[q, e], recv1.at[q, e]
        return send2.at[q, o % SIDE, e], recv2.at[q, o % SIDE, e]

    def arrived(self, q, phase, o, e):
        p = self.p
        away = {0: -1, 1: 1, 2: -2, 3: 2}[e]
        half = {0: None, 1: None, 2: 0, 3: 1}[e]
        step1, step2 = (away, 0) if phase == 1 else (o, away)
        return self.p, q, step1, step2, half

    def wait(self, q, phase, o, e):
        p, q, step1, step2, half = self.arrived(q, phase, o, e)
        dst = self.w.at[self.rows(q, p.core, step1, step2, half)]
        send, recv = self.sems(phase, q, o, e, self.send1, self.recv1, self.send2, self.recv2)
        remote(dst, dst, send, recv, {"mp": p.chip(0, 1)}).wait_recv()
        self.across(q, phase, o, e, p.core).start()

    def across(self, q, phase, o, e, core):
        p, q, step1, step2, half = self.arrived(q, phase, o, e)
        ref = self.w.at[self.rows(q, core, step1, step2, half)]
        send, recv = self.sems(phase, q, o, e, self.dsend1, self.drecv1, self.dsend2, self.drecv2)
        return remote(ref, ref, send, recv, {"dp": 1 - p.core})

    def begin(self):
        for q in (0, 1):
            self.copy(q, 1, 0, 0).start()
            self.copy(q, 1, 0, 1).start()
        for q in (0, 1):
            self.copy(q, 2, 0, 0).start()
            self.copy(q, 2, 0, 1).start()
        p = self.p
        self.w[pl.ds(pl.multiple_of(p.mp * self.depth, self.depth), self.depth), :] = self.shard[...]

    def run(self):
        for q in (0, 1):
            self.wait(q, 1, 0, 0)
            self.copy(q, 1, 0, 2).start()
            self.wait(q, 1, 0, 1)
            self.copy(q, 1, 0, 3).start()
        for q in (0, 1):
            for o in (-1, 1):
                self.copy(q, 2, o, 0).start()
                self.copy(q, 2, o, 1).start()
        for q in (0, 1):
            self.wait(q, 2, 0, 0)
            self.copy(q, 2, 0, 2).start()
            self.wait(q, 2, 0, 1)
            self.copy(q, 2, 0, 3).start()
        for q in (0, 1):
            self.wait(q, 1, 0, 2)
            self.wait(q, 1, 0, 3)
            self.copy(q, 2, 2, 0).start()
            self.copy(q, 2, 2, 1).start()
        for o in (-1, 1, 2):
            for q in (0, 1):
                self.wait(q, 2, o, 0)
                self.copy(q, 2, o, 2).start()
                self.wait(q, 2, o, 1)
                self.copy(q, 2, o, 3).start()
        for o in (0, -1, 1, 2):
            for q in (0, 1):
                self.wait(q, 2, o, 2)
                self.wait(q, 2, o, 3)
        other = 1 - self.p.core
        for q, phase, o, e in self.events():
            self.across(q, phase, o, e, other).wait_recv()

    def events(self):
        for q in (0, 1):
            for e in range(4):
                yield q, 1, 0, e
            for o in (0, -1, 1, 2):
                for e in range(4):
                    yield q, 2, o, e

    def drain(self):
        for q, phase, o, e in self.events():
            self.copy(q, phase, o, e).wait_send()
            self.across(q, phase, o, e, self.p.core).wait_send()


class Scatter:
    def __init__(self, place, refs, sems):
        self.p = place
        self.gs, self.gd, self.g, self.l1, self.l2, self.l3, self.l4 = refs
        self.dsend, self.drecv, self.send, self.recv, self.send2, self.recv2 = sems
        self.half = self.g.shape[3] // 2

    def cols(self, q):
        return pl.ds(q * self.half, self.half)

    def order(self, q):
        p = self.p
        c = p.x if q == 0 else p.y
        return [p.along(c, 2), p.along(c, 1), p.along(c, -1), c]

    def block(self, q, first, second):
        return (first, second) if q == 0 else (second, first)

    def ring1(self, q, steps):
        p = self.p
        return p.along(p.y if q == 0 else p.x, steps)

    def own1(self, q):
        return self.p.y if q == 0 else self.p.x

    def pair(self, q, first, low):
        if q == 0:
            return self.g.at[first, pl.ds(low, 2), :, self.cols(q)]
        return self.g.at[pl.ds(low, 2), first, :, self.cols(q)]

    def copy1(self, q, d):
        p = self.p
        src = self.pair(q, self.ring1(q, 2), 2 * d)
        return remote(src, self.l1.at[q, d], self.send.at[0, q, d], self.recv.at[0, q, d],
                      {"mp": p.chip(1 - q, 1 if d == 0 else -1)})

    def copy2(self, q, d, k):
        p = self.p
        to = 1 if d == 0 else -1
        a, b = self.block(q, self.ring1(q, to), self.order(q)[k])
        return remote(self.g.at[a, b, :, self.cols(q)], self.l2.at[q, d, k],
                      self.send2.at[q, d, k], self.recv2.at[q, d, k], {"mp": p.chip(1 - q, to)})

    def copy3(self, q, d):
        p = self.p
        a, b = self.block(q, self.own1(q), self.order(q)[0])
        n = self.g.shape[2] // 2
        return remote(self.g.at[a, b, pl.ds(d * n, n), self.cols(q)], self.l3.at[q, d],
                      self.send.at[1, q, d], self.recv.at[1, q, d],
                      {"mp": p.chip(q, 1 if d == 0 else -1)})

    def copy4(self, q, d):
        p = self.p
        a, b = self.block(q, self.own1(q), self.order(q)[1 + d])
        return remote(self.g.at[a, b, :, self.cols(q)], self.l4.at[q, d],
                      self.send.at[2, q, d], self.recv.at[2, q, d],
                      {"mp": p.chip(q, 1 if d == 0 else -1)})

    def exchange(self, k):
        at = self.p.along(self.p.y, (2, 1, -1, 0)[k])
        return remote(self.gs.at[at], self.gd.at[at], self.dsend.at[k], self.drecv.at[k],
                      {"dp": 1 - self.p.core})

    def products(self, left, right):
        p = self.p
        per = self.g.shape[1] * self.g.shape[2]
        total = self.g.shape[3]
        step = min(512, total)

        def product(core, at, store):
            start = pl.multiple_of(core * (SIDE * per) + at * per, per)
            rows = left(pl.ds(start, per))

            def tile(n, _):
                cols = pl.ds(pl.multiple_of(n * step, step), step)
                value = lax.dot_general(
                    rows, right(cols), (((0,), (0,)), ((), ())), preferred_element_type=F32
                )
                store(at, cols, value.reshape(SIDE, self.g.shape[2], step))
                return 0

            lax.fori_loop(0, total // step, tile, 0)

        def to_other(at, cols, value):
            self.gs[at, :, :, cols] = value.astype(BF16)

        def to_own(at, cols, value):
            self.g[at, :, :, cols] = (value + self.gd[at, :, :, cols].astype(F32)).astype(BF16)

        for k in range(SIDE):
            at = p.along(p.y, (2, 1, -1, 0)[k])
            product(1 - p.core, at, to_other)
            self.exchange(k).start()
        for k in range(SIDE):
            at = p.along(p.y, (2, 1, -1, 0)[k])
            self.exchange(k).wait_recv()
            product(p.core, at, to_own)
            if k == 0:
                self.copy1(0, 0).start()
                self.copy1(0, 1).start()
        self.copy1(1, 0).start()
        self.copy1(1, 1).start()

    def add(self, index, value):
        self.g[index] = (self.g[index].astype(F32) + value.astype(F32)).astype(BF16)

    def run(self, finish):
        n = self.g.shape[2] // 2
        for d in (0, 1):
            for q in (0, 1):
                self.copy1(q, d).wait_recv()
                first = self.ring1(q, 1 if d == 0 else -1)
                for k in (0, 1):
                    a, b = self.block(q, first, 2 * d + k)
                    self.add((a, b, slice(None), self.cols(q)), self.l1[q, d, k])
                for k in range(SIDE):
                    self.copy2(q, d, k).start()
        for k in range(SIDE):
            for q in (0, 1):
                self.copy2(q, 0, k).wait_recv()
                self.copy2(q, 1, k).wait_recv()
                a, b = self.block(q, self.own1(q), self.order(q)[k])
                self.add(
                    (a, b, slice(None), self.cols(q)),
                    self.l2[q, 0, k].astype(F32) + self.l2[q, 1, k].astype(F32),
                )
                if k == 0:
                    self.copy3(q, 0).start()
                    self.copy3(q, 1).start()
                if k in (1, 2):
                    d = k - 1
                    self.copy3(q, d).wait_recv()
                    self.add((a, b, pl.ds(d * n, n), self.cols(q)), self.l3[q, d])
                    self.copy4(q, d).start()
        for q in (0, 1):
            self.copy4(q, 0).wait_recv()
            self.copy4(q, 1).wait_recv()
            a, b = self.block(q, self.own1(q), self.order(q)[3])
            finish(
                q,
                self.g[a, b, :, self.cols(q)].astype(F32)
                + self.l4[q, 0].astype(F32)
                + self.l4[q, 1].astype(F32),
            )

    def drain(self):
        for k in range(SIDE):
            self.exchange(k).wait_send()
        for q in (0, 1):
            for d in (0, 1):
                self.copy1(q, d).wait_send()
                self.copy3(q, d).wait_send()
                self.copy4(q, d).wait_send()
                for k in range(SIDE):
                    self.copy2(q, d, k).wait_send()


def step_kernel(sections, *refs):
    (
        inputs, tangents, targets, target_jac, mask, batch_order, encoder, shard, head,
        o_layer, o_head, o_loss,
        w, xin, xout, mix, cot, pin, pout, pre, thb, cin, cpin, cout, cpout, mixp, cotp,
        count_out, count_in, loss_out, loss_in, loss_sum, loss_land, head_out, head_land,
        fsend, frecv, bsend, brecv,
        gsend1, grecv1, gsend2, grecv2, dsend1, drecv1, dsend2, drecv2,
        csend, crecv, lsend, lrecv, zsend, zrecv,
        *scatter,
    ) = refs
    layer_refs, layer_sems = scatter[:7], scatter[7:13]
    head_refs, head_sems = scatter[13:20], scatter[20:26]
    n_mb, rows, width = xin.shape
    rank = cin.shape[1]
    out_width = head.shape[1]
    tile = width // PIECES
    place = Place(sections)
    s, core, first, last = place.s, place.core, place.first, place.last
    chips = SIDE * SIDE

    enter(place)
    gather = Gather(place, shard, w, (gsend1, grecv1, gsend2, grecv2, dsend1, drecv1, dsend2, drecv2))
    gather.begin()

    def totals_and_where():
        totals = 1.0 + jnp.sum(mask[...].astype(F32), axis=1, keepdims=True)
        where = lax.broadcasted_iota(jnp.int32, (n_mb, n_mb), 0) == jnp.broadcast_to(
            batch_order[...], (n_mb, n_mb)
        )
        return totals, where.astype(F32)

    def count_copy(step, receiving):
        other = lax.rem(place.mp + step, chips)
        source = lax.rem(place.mp + chips - step, chips)
        slot = source if receiving else place.mp
        return remote(count_out, count_in.at[slot], csend.at[step], crecv.at[step], {"mp": other})

    @pl.when(last)
    def _():
        totals, where = totals_and_where()
        count_out[...] = jnp.zeros_like(count_out)
        count_out[0:1, 0:n_mb] = jnp.sum(where * totals, axis=0, keepdims=True)
        count_in[place.mp] = count_out[...]
        lax.fori_loop(1, chips, lambda i, _: (count_copy(i, False).start(), 0)[1], 0)

    @pl.when(first)
    def _():
        primal = inputs[...].astype(F32)
        for m in range(n_mb):
            lhs = jnp.concatenate(
                [tangents[m], first_row(primal[m : m + 1], rows - rank).astype(BF16)], axis=0
            )
            lifted = jnp.dot(lhs, encoder[...], preferred_element_type=F32).astype(BF16)
            xin[m] = lifted
            pin[m] = lifted[rank:].astype(F32)[0:1]

    gather.run()

    def fcopy(m, j):
        cols = pl.ds(j * tile, tile)
        return remote(
            xout.at[m, pl.ds(0, rank), cols], xin.at[m, pl.ds(0, rank), cols],
            fsend.at[m, j], frecv.at[m, j], {"section": place.nxt},
        )

    def fpcopy(m):
        return remote(
            pout.at[m], pin.at[m], fsend.at[m, PIECES], frecv.at[m, PIECES], {"section": place.nxt}
        )

    def bcopy(m, j):
        cols = pl.ds(j * tile, tile)
        return remote(
            cout.at[m, :, cols], cin.at[m, :, cols],
            bsend.at[m, j], brecv.at[m, j], {"section": place.prv},
        )

    def bpcopy(m):
        return remote(
            cpout.at[m], cpin.at[m], bsend.at[m, PIECES], brecv.at[m, PIECES], {"section": place.prv}
        )

    def forward(m, _):
        @pl.when(jnp.logical_not(first))
        def _():
            for j in range(PIECES):
                fcopy(m, j).wait_recv()
            fpcopy(m).wait_recv()
            xin[m, pl.ds(rank, rows - rank), :] = first_row(pin[m], rows - rank).astype(BF16)

        for j in range(PIECES):
            cols = pl.ds(j * tile, tile)
            acc = jnp.dot(xin[m], w[:, cols], preferred_element_type=F32)
            th = jnp.tanh(acc[rank : rank + 1, :])
            slope = 1.0 - th * th
            tangent = acc[:rank, :]
            pre[m, :, cols] = tangent
            thb[m, :, cols] = th
            moved = xin[m, pl.ds(0, rank), cols].astype(F32) + slope * tangent
            xout[m, pl.ds(0, rank), cols] = moved.astype(BF16)
            primal = (pin[m, :, cols] + th).astype(BF16).astype(F32)
            pout[m, :, cols] = primal
            xout[m, pl.ds(rank, rows - rank), cols] = first_row(primal, rows - rank).astype(BF16)

            @pl.when(jnp.logical_not(last))
            def _():
                fcopy(m, j).start()

        @pl.when(jnp.logical_not(last))
        def _():
            fpcopy(m).start()

        return 0

    lax.fori_loop(0, n_mb, forward, 0)

    def loss_copy(step, receiving):
        plane = 2 * chips
        me = core * chips + place.mp
        other = lax.rem(me + step, plane)
        source = lax.rem(me + plane - step, plane)
        slot = source if receiving else me
        return remote(
            loss_out, loss_in.at[slot], lsend.at[step], lrecv.at[step],
            {"dp": other // chips, "mp": lax.rem(other, chips)},
        )

    @pl.when(last)
    def _():
        lax.fori_loop(1, chips, lambda i, _: (count_copy(i, True).wait_recv(), 0)[1], 0)
        totals, where = totals_and_where()
        counts = jnp.sum(count_in[...], axis=0)[0:1, 0:n_mb]
        inverse = 1.0 / jnp.sum(where * counts, axis=1, keepdims=True)
        row = lax.broadcasted_iota(jnp.int32, (rows, 1), 0)
        ranks = totals.astype(jnp.int32) - 1
        step = min(256, out_width)
        total = jnp.zeros((1, 1), F32)
        for n in range(out_width // step):
            cols = pl.ds(n * step, step)
            outputs = jnp.dot(
                xout[...].reshape(n_mb * rows, width), head[:, cols], preferred_element_type=F32
            )
            primal_wanted = targets[:, cols].astype(F32)
            for m in range(n_mb):
                wanted = jnp.concatenate(
                    [
                        target_jac[m, :, cols].astype(F32),
                        first_row(primal_wanted[m : m + 1], rows - rank),
                    ],
                    axis=0,
                )
                present = jnp.logical_or(row < ranks[m : m + 1], row == rank)
                scale = jnp.where(present, inverse[m : m + 1], 0.0)
                mismatch = outputs[m * rows : (m + 1) * rows] - wanted
                weighted = scale * mismatch
                total = total + jnp.sum(
                    jnp.sum(weighted * mismatch, axis=0, keepdims=True), axis=1, keepdims=True
                )
                rounded = (2.0 * weighted).astype(BF16)
                cot[m, :, cols] = rounded
                cotp[m, :, cols] = rounded[rank:].astype(F32)[0:1]
        loss_out[...] = jnp.broadcast_to(total, loss_out.shape)
        loss_in[core * chips + place.mp] = loss_out[...]
        lax.fori_loop(1, 2 * chips, lambda i, _: (loss_copy(i, False).start(), 0)[1], 0)
        for n in range(width // step):
            cols = pl.ds(n * step, step)
            grads = lax.dot_general(
                cot[...].reshape(n_mb * rows, out_width), head[cols, :], (((1,), (1,)), ((), ())),
                preferred_element_type=F32,
            ).astype(BF16)
            for m in range(n_mb):
                cin[m, :, cols] = grads[m * rows : m * rows + rank, :]
                cpin[m, :, cols] = grads[m * rows + rank : m * rows + rows, :].astype(F32)[0:1]

    def backward(m, _):
        @pl.when(jnp.logical_not(last))
        def _():
            for j in range(PIECES):
                bcopy(m, j).wait_recv()
            bpcopy(m).wait_recv()

        for j in range(PIECES):
            cols = pl.ds(j * tile, tile)
            upstream = cin[m, :, cols].astype(F32)
            th = thb[m, :, cols]
            slope = 1.0 - th * th
            mix[m, pl.ds(0, rank), cols] = (upstream * slope).astype(BF16)
            total = jnp.sum(upstream * pre[m, :, cols], axis=0, keepdims=True)
            primal = cpin[m, :, cols] * slope - 2.0 * total * th * slope
            mixp[m, :, cols] = primal
            mix[m, pl.ds(rank, rows - rank), cols] = first_row(primal, rows - rank).astype(BF16)

        @pl.when(jnp.logical_not(first))
        def _():
            for j in range(PIECES):
                cols = pl.ds(j * tile, tile)
                back = lax.dot_general(
                    mix[m], w[cols, :], (((1,), (1,)), ((), ())), preferred_element_type=F32
                )
                cout[m, :, cols] = (cin[m, :, cols].astype(F32) + back[:rank]).astype(BF16)
                cpout[m, :, cols] = (
                    (cpin[m, :, cols] + back[rank : rank + 1]).astype(BF16).astype(F32)
                )
                bcopy(m, j).start()
            bpcopy(m).start()

        return 0

    lax.fori_loop(0, n_mb, backward, 0)

    def compact(tangent, primal):
        def take(cols):
            block = tangent[:, pl.ds(0, rank), cols]
            rest = stacked_rows(lambda m: primal[m, :, cols], n_mb, 16, block.shape[2])
            return jnp.concatenate(
                [block.reshape(n_mb * rank, block.shape[2]), rest.astype(BF16)], axis=0
            )

        return take

    def section_copy(step, what):
        other = lax.rem(place.s + step, sections)
        if what == 0:
            return remote(head_out.at[other], head_land, zsend.at[0, step], zrecv.at[0], {"section": other})
        return remote(loss_sum, loss_land, zsend.at[1, step], zrecv.at[1], {"section": other})

    heads = Scatter(place, head_refs, head_sems)

    @pl.when(last)
    def _():
        heads.products(compact(xout, pout), compact(cot, cotp))

        def finish(q, value):
            per = out_width // sections
            for k in range(heads.half // per):
                head_out[q * (heads.half // per) + k] = value[:, k * per : (k + 1) * per]

        heads.run(finish)
        lax.fori_loop(1, 2 * chips, lambda i, _: (loss_copy(i, True).wait_recv(), 0)[1], 0)
        loss_sum[...] = jnp.sum(loss_in[...], axis=0)

        def spread(i, _):
            section_copy(i, 0).start()
            section_copy(i, 1).start()
            return 0

        lax.fori_loop(1, sections, spread, 0)
        o_head[...] = head_out[sections - 1]
        o_loss[...] = loss_sum[...]

    sums = Scatter(place, layer_refs, layer_sems)
    sums.products(compact(xin, pin), compact(mix, mixp))

    def finish_layer(q, value):
        o_layer[:, pl.ds(q * sums.half, sums.half)] = value

    sums.run(finish_layer)

    @pl.when(jnp.logical_not(last))
    def _():
        section_copy(1, 0).wait_recv()
        section_copy(1, 1).wait_recv()
        o_head[...] = head_land[...]
        o_loss[...] = loss_land[...]

    def drain(m, _):
        @pl.when(jnp.logical_not(last))
        def _():
            for j in range(PIECES):
                fcopy(m, j).wait_send()
            fpcopy(m).wait_send()

        @pl.when(jnp.logical_not(first))
        def _():
            for j in range(PIECES):
                bcopy(m, j).wait_send()
            bpcopy(m).wait_send()

        return 0

    lax.fori_loop(0, n_mb, drain, 0)
    gather.drain()
    sums.drain()

    @pl.when(last)
    def _():
        heads.drain()
        lax.fori_loop(1, chips, lambda i, _: (count_copy(i, False).wait_send(), 0)[1], 0)
        lax.fori_loop(1, 2 * chips, lambda i, _: (loss_copy(i, False).wait_send(), 0)[1], 0)

        def spread(i, _):
            section_copy(i, 0).wait_send()
            section_copy(i, 1).wait_send()
            return 0

        lax.fori_loop(1, sections, spread, 0)


def scatter_scratch(rows, cols):
    half = cols // 2
    dma = pltpu.SemaphoreType.DMA
    part = (SIDE, SIDE, rows, cols)
    return [
        pltpu.VMEM(part, BF16),
        pltpu.VMEM(part, BF16),
        pltpu.VMEM(part, BF16),
        pltpu.VMEM((2, 2, 2, rows, half), BF16),
        pltpu.VMEM((2, 2, SIDE, rows, half), BF16),
        pltpu.VMEM((2, 2, rows // 2, half), BF16),
        pltpu.VMEM((2, 2, rows, half), BF16),
        dma((SIDE,)), dma((SIDE,)),
        dma((3, 2, 2)), dma((3, 2, 2)),
        dma((2, 2, SIDE)), dma((2, 2, SIDE)),
    ]


def local(
    inputs, tangents, targets, target_jac, rank_mask, batch_order, encoder, layers, head_weight
):
    n_mb, rank, _ = tangents.shape
    width = layers.shape[2]
    out_width = head_weight.shape[1]
    sections = lax.axis_size("section")
    chips = SIDE * SIDE
    own = width // (2 * chips)
    per = out_width // sections
    dma = pltpu.SemaphoreType.DMA
    vmem = pl.BlockSpec(memory_space=pltpu.VMEM)
    row = pltpu.VMEM((n_mb, 1, width), F32)
    block = pltpu.VMEM((n_mb, ROWS, width), BF16)
    send = pltpu.VMEM((n_mb, rank, width), BF16)
    grad_layer, grad_head, loss = pl.pallas_call(
        functools.partial(step_kernel, sections),
        out_shape=(
            jax.ShapeDtypeStruct((own, width), F32),
            jax.ShapeDtypeStruct((own, per), F32),
            jax.ShapeDtypeStruct((8, 128), F32),
        ),
        in_specs=[vmem] * 9,
        out_specs=(vmem,) * 3,
        scratch_shapes=[
            pltpu.VMEM((width, width), BF16),
            block, block, block,
            pltpu.VMEM((n_mb, ROWS, out_width), BF16),
            row, row,
            pltpu.VMEM((n_mb, rank, width), F32),
            row, send, row, send, row, row,
            pltpu.VMEM((n_mb, 1, out_width), F32),
            pltpu.VMEM((8, 128), F32),
            pltpu.VMEM((chips, 8, 128), F32),
            pltpu.VMEM((8, 128), F32),
            pltpu.VMEM((2 * chips, 8, 128), F32),
            pltpu.VMEM((8, 128), F32),
            pltpu.VMEM((8, 128), F32),
            pltpu.VMEM((sections, own, per), F32),
            pltpu.VMEM((own, per), F32),
            dma((n_mb, PIECES + 1)), dma((n_mb, PIECES + 1)),
            dma((n_mb, PIECES + 1)), dma((n_mb, PIECES + 1)),
            dma((2, 4)), dma((2, 4)), dma((2, SIDE, 4)), dma((2, SIDE, 4)),
            dma((2, 4)), dma((2, 4)), dma((2, SIDE, 4)), dma((2, SIDE, 4)),
            dma((chips,)), dma((chips,)),
            dma((2 * chips,)), dma((2 * chips,)),
            dma((2, sections)), dma((2,)),
            *scatter_scratch(own, width),
            *scatter_scratch(own, out_width),
        ],
        compiler_params=pltpu.CompilerParams(
            collective_id=0, has_side_effects=True, vmem_limit_bytes=67043328
        ),
        name="step",
    )(
        inputs, tangents, targets, target_jac, rank_mask, batch_order, encoder, layers[0],
        head_weight,
    )
    loss_value = loss[0, 0] / (lax.axis_size("dp") * n_mb * out_width)
    return grad_layer[None], grad_head, loss_value


def solution(mesh):
    in_specs = (
        P(("dp", "mp"), None),
        P(("dp", "mp"), None, None),
        P(("dp", "mp"), None),
        P(("dp", "mp"), None, None),
        P(("dp", "mp"), None),
        P(("dp", "mp"), None),
        P(),
        P("section", "mp", None),
        P(),
    )
    out_specs = (P("section", ("dp", "mp"), None), P(("dp", "mp"), "section"), P())
    return jax.shard_map(local, mesh=mesh, in_specs=in_specs, out_specs=out_specs, check_vma=False)
```

time: 396 us -> 208 us (0.53)
  blocking collectives: 115 us -> 0 us
  Pallas kernels: 126 us -> 201 us
  waiting for transfers between devices: 66.1 us -> 0 us
  local copies, waits for them, and re-layouts: 32.1 us -> 4.43 us
  other arithmetic: 21.1 us -> 0 us
  between operations: 16 us -> 2.43 us
  matrix products: 9.57 us -> 0 us
  starting transfers between devices: 6.79 us -> 0 us
    psum x2 -> x0, blocking collectives: 115 us -> none  [the longest x1 80.3 us: local(): loss_sum = lax.psum(loss[0, 0], ('dp', 'section', 'mp'))]
    pallas_call x1, Pallas kernels: 126 us -> 201 us  [local(): pl.pallas_call(functools.partial(step_kernel, sections), out_shape=(jax.S...]
    all_gather x1 -> x0, waiting for transfers between devices: 32.4 us -> none  [local(): weight = lax.all_gather(layers[0], 'mp', axis=0, tiled=True)]
    unnamed x3 -> x0, waiting for transfers between devices: 30.1 us -> none
    unnamed x19 -> x2, local copies, waits for them, and re-layouts: 25.6 us -> 3.25 us
    concatenate x3 -> x0, other arithmetic: 15.5 us -> none  [the longest x1 14.4 us: local(): jnp.concatenate([grad_layer.astype(jnp.bfloat16), grad_head.astype(jnp.bf...]
    dot_general x3 -> x0, matrix products: 9.57 us -> none  [the longest x1 4.81 us: local(): grad_layer = jnp.dot(flat(x_in).T, flat(mix), preferred_element_type=f32)]
    all_to_all x1 -> x0, starting transfers between devices: 6.72 us -> none  [local(): lax.all_to_all(parts, 'section', split_axis=0, concat_axis=0, tiled=True)]
  transfers between devices with their start and end apart: 3 -> 0, of which waited for: 3 -> 0; matrix products, arithmetic and copies ran while one was open for 5% -> 0% of each run, Pallas kernels for 0% -> 0%
where the time goes in v2:
time: 208 us
  Pallas kernels  201 us (97%)
  local copies, waits for them, and re-layouts  4.43 us (2%)
  between operations  2.43 us (1%)
    pallas_call x1, Pallas kernels, local(): pl.pallas_call(functools.partial(step_kernel, sections), out_shape=(jax.S...  201 us

profile of v2, /device:TPU:1, one launch (start us, length us, event | category | flops | bytes accessed | tf_op | source)
XLA Modules:
  0.0 207.6 jit_solution(3926716586718912779)
XLA Ops:
  0.6 200.8 %step.1 = (f32[64,2048]{1,0:T(8,128)}, f32[64,128]{1,0:T(8,128)}, f32[8,128]{1,0:T(8,128)}) custom-call(bf16[6,512]{1,0:T(8,128)(2,1)} %refs_0_.1, bf16[6,32,512]{2,1,0:T(8,128)(2,1)} %refs_1_.1, bf16[6,1024]{1,0:T(8,128)(2,1)} %refs_2_.1, bf16[6,32,1024]{2,1,0:T(8,128)(2,1)} %refs_3_.1, s32[6,32]{1,0:T(8,128)} %refs_4_.1, s32[1,6]{1,0:T(1,128)} %refs_5_.1, ...), custom_call_target="tpu_custom_call" | custom-call | tf_op jit(solution)/shard_map/step/pallas_call | solution.py:688
  201.4 1.2 slice.3
  203.2 1.9 copy.14
  205.1 1.4 copy.15

commit v3 on v2

--- a/solution.py
+++ b/solution.py
@@ -83,8 +83,7 @@
 class Gather:
     def __init__(self, place, shard, w, sems):
         self.p, self.shard, self.w = place, shard, w
-        self.send1, self.recv1, self.send2, self.recv2 = sems[:4]
-        self.dsend1, self.drecv1, self.dsend2, self.drecv2 = sems[4:]
+        self.sent, self.recv1, self.recv2, self.dsent, self.dgot = sems
         self.depth = shard.shape[0]
         self.piece = self.depth // 4
 
@@ -110,13 +109,10 @@
         src = dst
         if step1 == 0 and step2 == 0:
             src = self.shard.at[pl.ds(pl.multiple_of(p.core * (2 * self.piece) + q * self.piece, self.piece), self.piece)]
-        send, recv = self.sems(phase, q, o, e, self.send1, self.recv1, self.send2, self.recv2)
-        return remote(src, dst, send, recv, {"mp": p.chip(axis, to)})
-
-    def sems(self, phase, q, o, e, send1, recv1, send2, recv2):
-        if phase == 1:
-            return send1.at[q, e], recv1.at[q, e]
-        return send2.at[q, o % SIDE, e], recv2.at[q, o % SIDE, e]
+        return remote(src, dst, self.sent, self.recv(phase, q, o, e), {"mp": p.chip(axis, to)})
+
+    def recv(self, phase, q, o, e):
+        return self.recv1.at[q, e] if phase == 1 else self.recv2.at[q, o % SIDE, e]
 
     def arrived(self, q, phase, o, e):
         p = self.p
@@ -128,15 +124,12 @@
     def wait(self, q, phase, o, e):
         p, q, step1, step2, half = self.arrived(q, phase, o, e)
         dst = self.w.at[self.rows(q, p.core, step1, step2, half)]
-        send, recv = self.sems(phase, q, o, e, self.send1, self.recv1, self.send2, self.recv2)
-        remote(dst, dst, send, recv, {"mp": p.chip(0, 1)}).wait_recv()
-        self.across(q, phase, o, e, p.core).start()
-
-    def across(self, q, phase, o, e, core):
-        p, q, step1, step2, half = self.arrived(q, phase, o, e)
-        ref = self.w.at[self.rows(q, core, step1, step2, half)]
-        send, recv = self.sems(phase, q, o, e, self.dsend1, self.drecv1, self.dsend2, self.drecv2)
-        return remote(ref, ref, send, recv, {"dp": 1 - p.core})
+        remote(dst, dst, self.sent, self.recv(phase, q, o, e), {"mp": p.chip(0, 1)}).wait_recv()
+        remote(dst, dst, self.dsent, self.dgot, {"dp": 1 - p.core}).start()
+
+    def all_of(self, send, recv):
+        ref = self.w.at[pl.ds(0, (SIDE * SIDE - 1) * 2 * self.piece)]
+        return remote(ref, ref, send, recv, {"dp": 1 - self.p.core})
 
     def begin(self):
         for q in (0, 1):
@@ -148,7 +141,7 @@
         p = self.p
         self.w[pl.ds(pl.multiple_of(p.mp * self.depth, self.depth), self.depth), :] = self.shard[...]
 
-    def run(self):
+    def run(self, meanwhile):
         for q in (0, 1):
             self.wait(q, 1, 0, 0)
             self.copy(q, 1, 0, 2).start()
@@ -158,6 +151,7 @@
             for o in (-1, 1):
                 self.copy(q, 2, o, 0).start()
                 self.copy(q, 2, o, 1).start()
+        meanwhile()
         for q in (0, 1):
             self.wait(q, 2, 0, 0)
             self.copy(q, 2, 0, 2).start()
@@ -178,29 +172,18 @@
             for q in (0, 1):
                 self.wait(q, 2, o, 2)
                 self.wait(q, 2, o, 3)
-        other = 1 - self.p.core
-        for q, phase, o, e in self.events():
-            self.across(q, phase, o, e, other).wait_recv()
-
-    def events(self):
-        for q in (0, 1):
-            for e in range(4):
-                yield q, 1, 0, e
-            for o in (0, -1, 1, 2):
-                for e in range(4):
-                    yield q, 2, o, e
+        self.all_of(self.dsent, self.dgot).wait_recv()
 
     def drain(self):
-        for q, phase, o, e in self.events():
-            self.copy(q, phase, o, e).wait_send()
-            self.across(q, phase, o, e, self.p.core).wait_send()
+        self.all_of(self.sent, self.dgot).wait_send()
+        self.all_of(self.dsent, self.dgot).wait_send()
 
 
 class Scatter:
     def __init__(self, place, refs, sems):
         self.p = place
-        self.gs, self.gd, self.g, self.l1, self.l2, self.l3, self.l4 = refs
-        self.dsend, self.drecv, self.send, self.recv, self.send2, self.recv2 = sems
+        self.gs, self.gd, self.g, self.l1, self.l2, self.l3, self.l4, self.turned = refs
+        self.sent, self.drecv, self.recv, self.recv2 = sems
         self.half = self.g.shape[3] // 2
 
     def cols(self, q):
@@ -229,7 +212,7 @@
     def copy1(self, q, d):
         p = self.p
         src = self.pair(q, self.ring1(q, 2), 2 * d)
-        return remote(src, self.l1.at[q, d], self.send.at[0, q, d], self.recv.at[0, q, d],
+        return remote(src, self.l1.at[q, d], self.sent.at[1], self.recv.at[0, q, d],
                       {"mp": p.chip(1 - q, 1 if d == 0 else -1)})
 
     def copy2(self, q, d, k):
@@ -237,26 +220,26 @@
         to = 1 if d == 0 else -1
         a, b = self.block(q, self.ring1(q, to), self.order(q)[k])
         return remote(self.g.at[a, b, :, self.cols(q)], self.l2.at[q, d, k],
-                      self.send2.at[q, d, k], self.recv2.at[q, d, k], {"mp": p.chip(1 - q, to)})
+                      self.sent.at[2], self.recv2.at[q, d, k], {"mp": p.chip(1 - q, to)})
 
     def copy3(self, q, d):
         p = self.p
         a, b = self.block(q, self.own1(q), self.order(q)[0])
         n = self.g.shape[2] // 2
         return remote(self.g.at[a, b, pl.ds(d * n, n), self.cols(q)], self.l3.at[q, d],
-                      self.send.at[1, q, d], self.recv.at[1, q, d],
+                      self.sent.at[3], self.recv.at[1, q, d],
                       {"mp": p.chip(q, 1 if d == 0 else -1)})
 
     def copy4(self, q, d):
         p = self.p
         a, b = self.block(q, self.own1(q), self.order(q)[1 + d])
         return remote(self.g.at[a, b, :, self.cols(q)], self.l4.at[q, d],
-                      self.send.at[2, q, d], self.recv.at[2, q, d],
+                      self.sent.at[4], self.recv.at[2, q, d],
                       {"mp": p.chip(q, 1 if d == 0 else -1)})
 
     def exchange(self, k):
         at = self.p.along(self.p.y, (2, 1, -1, 0)[k])
-        return remote(self.gs.at[at], self.gd.at[at], self.dsend.at[k], self.drecv.at[k],
+        return remote(self.gs.at[at], self.gd.at[at], self.sent.at[0], self.drecv.at[k],
                       {"dp": 1 - self.p.core})
 
     def products(self, left, right):
@@ -267,13 +250,11 @@
 
         def product(core, at, store):
             start = pl.multiple_of(core * (SIDE * per) + at * per, per)
-            rows = left(pl.ds(start, per))
+            self.turned[...] = left(pl.ds(start, per)).T
 
             def tile(n, _):
                 cols = pl.ds(pl.multiple_of(n * step, step), step)
-                value = lax.dot_general(
-                    rows, right(cols), (((0,), (0,)), ((), ())), preferred_element_type=F32
-                )
+                value = jnp.dot(self.turned[...], right(cols), preferred_element_type=F32)
                 store(at, cols, value.reshape(SIDE, self.g.shape[2], step))
                 return 0
 
@@ -342,30 +323,24 @@
             )
 
     def drain(self):
-        for k in range(SIDE):
-            self.exchange(k).wait_send()
-        for q in (0, 1):
-            for d in (0, 1):
-                self.copy1(q, d).wait_send()
-                self.copy3(q, d).wait_send()
-                self.copy4(q, d).wait_send()
-                for k in range(SIDE):
-                    self.copy2(q, d, k).wait_send()
-
-
-def step_kernel(sections, *refs):
+        for n, ref in enumerate((self.gd, self.l1, self.l2, self.l3, self.l4)):
+            remote(ref, ref, self.sent.at[n], self.drecv.at[0], {"dp": 1 - self.p.core}).wait_send()
+
+
+def step_kernel(sections, loss_scale, *refs):
     (
-        inputs, tangents, targets, target_jac, mask, batch_order, encoder, shard, head,
+        h_inputs, h_tangents, h_targets, h_target_jac, mask, batch_order, h_encoder, h_shard, h_head,
         o_layer, o_head, o_loss,
-        w, xin, xout, mix, cot, pin, pout, pre, thb, cin, cpin, cout, cpout, mixp, cotp,
+        inputs, tangents, targets, target_jac, encoder, shard, head,
+        w, wt, xin, xout, mix, cot, pin, pout, pre, thb, cin, cpin, cout, cpout, mixp, cotp,
         count_out, count_in, loss_out, loss_in, loss_sum, loss_land, head_out, head_land,
-        fsend, frecv, bsend, brecv,
-        gsend1, grecv1, gsend2, grecv2, dsend1, drecv1, dsend2, drecv2,
+        loads, relayed, frecv, brecv,
+        gsent, grecv1, grecv2, dsent, dgot,
         csend, crecv, lsend, lrecv, zsend, zrecv,
         *scatter,
     ) = refs
-    layer_refs, layer_sems = scatter[:7], scatter[7:13]
-    head_refs, head_sems = scatter[13:20], scatter[20:26]
+    layer_refs, layer_sems = scatter[:8], scatter[8:12]
+    head_refs, head_sems = scatter[12:20], scatter[20:24]
     n_mb, rows, width = xin.shape
     rank = cin.shape[1]
     out_width = head.shape[1]
@@ -374,8 +349,18 @@
     s, core, first, last = place.s, place.core, place.first, place.last
     chips = SIDE * SIDE
 
+    def load(n):
+        pairs = (
+            (h_shard, shard), (h_inputs, inputs), (h_tangents, tangents), (h_encoder, encoder),
+            (h_targets, targets), (h_target_jac, target_jac), (h_head, head),
+        )
+        return pltpu.make_async_copy(pairs[n][0], pairs[n][1], loads.at[n])
+
+    for n in range(7):
+        load(n).start()
     enter(place)
-    gather = Gather(place, shard, w, (gsend1, grecv1, gsend2, grecv2, dsend1, drecv1, dsend2, drecv2))
+    load(0).wait()
+    gather = Gather(place, shard, w, (gsent, grecv1, grecv2, dsent, dgot))
     gather.begin()
 
     def totals_and_where():
@@ -385,11 +370,10 @@
         )
         return totals, where.astype(F32)
 
-    def count_copy(step, receiving):
+    def count_copy(step):
         other = lax.rem(place.mp + step, chips)
-        source = lax.rem(place.mp + chips - step, chips)
-        slot = source if receiving else place.mp
-        return remote(count_out, count_in.at[slot], csend.at[step], crecv.at[step], {"mp": other})
+        slot = place.mp
+        return remote(count_out, count_in.at[slot], csend.at[0], crecv.at[0], {"mp": other})
 
     @pl.when(last)
     def _():
@@ -397,50 +381,80 @@
         count_out[...] = jnp.zeros_like(count_out)
         count_out[0:1, 0:n_mb] = jnp.sum(where * totals, axis=0, keepdims=True)
         count_in[place.mp] = count_out[...]
-        lax.fori_loop(1, chips, lambda i, _: (count_copy(i, False).start(), 0)[1], 0)
-
-    @pl.when(first)
-    def _():
-        primal = inputs[...].astype(F32)
-        for m in range(n_mb):
-            lhs = jnp.concatenate(
-                [tangents[m], first_row(primal[m : m + 1], rows - rank).astype(BF16)], axis=0
-            )
-            lifted = jnp.dot(lhs, encoder[...], preferred_element_type=F32).astype(BF16)
-            xin[m] = lifted
-            pin[m] = lifted[rank:].astype(F32)[0:1]
-
-    gather.run()
+        lax.fori_loop(1, chips, lambda i, _: (count_copy(i).start(), 0)[1], 0)
+
+    def all_counts():
+        ref = count_in.at[pl.ds(0, chips - 1)]
+        return remote(ref, ref, csend.at[0], crecv.at[0], {"dp": 1 - core})
+
+    def all_losses():
+        ref = loss_in.at[pl.ds(0, 2 * chips - 1)]
+        return remote(ref, ref, lsend.at[0], lrecv.at[0], {"dp": 1 - core})
+
+    def encode():
+        for n in range(1, 7):
+            load(n).wait()
+
+        @pl.when(first)
+        def _():
+            primal = inputs[...].astype(F32)
+            for m in range(n_mb):
+                lhs = jnp.concatenate(
+                    [tangents[m], first_row(primal[m : m + 1], rows - rank).astype(BF16)], axis=0
+                )
+                lifted = jnp.dot(lhs, encoder[...], preferred_element_type=F32).astype(BF16)
+                xin[m] = lifted
+                pin[m] = lifted[rank:].astype(F32)[0:1]
+
+    gather.run(encode)
+
+    def turn_layer():
+        step = min(512, width)
+        count = width // step
+
+        def turn(n, _):
+            a = pl.ds(pl.multiple_of((n // count) * step, step), step)
+            b = pl.ds(pl.multiple_of(lax.rem(n, count) * step, step), step)
+            wt[b, a] = w[a, b].T
+            return 0
+
+        lax.fori_loop(0, count * count, turn, 0)
+
+    late = s >= sections // 2
+
+    @pl.when(late)
+    def _():
+        turn_layer()
 
     def fcopy(m, j):
         cols = pl.ds(j * tile, tile)
         return remote(
             xout.at[m, pl.ds(0, rank), cols], xin.at[m, pl.ds(0, rank), cols],
-            fsend.at[m, j], frecv.at[m, j], {"section": place.nxt},
+            relayed.at[0], frecv.at[m, 0], {"section": place.nxt},
         )
 
     def fpcopy(m):
         return remote(
-            pout.at[m], pin.at[m], fsend.at[m, PIECES], frecv.at[m, PIECES], {"section": place.nxt}
+            pout.at[m], pin.at[m], relayed.at[1], frecv.at[m, 1], {"section": place.nxt}
         )
 
     def bcopy(m, j):
         cols = pl.ds(j * tile, tile)
         return remote(
             cout.at[m, :, cols], cin.at[m, :, cols],
-            bsend.at[m, j], brecv.at[m, j], {"section": place.prv},
+            relayed.at[2], brecv.at[m, 0], {"section": place.prv},
         )
 
     def bpcopy(m):
         return remote(
-            cpout.at[m], cpin.at[m], bsend.at[m, PIECES], brecv.at[m, PIECES], {"section": place.prv}
+            cpout.at[m], cpin.at[m], relayed.at[3], brecv.at[m, 1], {"section": place.prv}
         )
 
     def forward(m, _):
         @pl.when(jnp.logical_not(first))
         def _():
-            for j in range(PIECES):
-                fcopy(m, j).wait_recv()
+            ref = xin.at[m, pl.ds(0, rank)]
+            remote(ref, ref, relayed.at[0], frecv.at[m, 0], {"section": place.nxt}).wait_recv()
             fpcopy(m).wait_recv()
             xin[m, pl.ds(rank, rows - rank), :] = first_row(pin[m], rows - rank).astype(BF16)
 
@@ -470,20 +484,23 @@
 
     lax.fori_loop(0, n_mb, forward, 0)
 
-    def loss_copy(step, receiving):
+    @pl.when(jnp.logical_and(jnp.logical_not(late), jnp.logical_not(first)))
+    def _():
+        turn_layer()
+
+    def loss_copy(step):
         plane = 2 * chips
         me = core * chips + place.mp
         other = lax.rem(me + step, plane)
-        source = lax.rem(me + plane - step, plane)
-        slot = source if receiving else me
+        slot = me
         return remote(
-            loss_out, loss_in.at[slot], lsend.at[step], lrecv.at[step],
+            loss_out, loss_in.at[slot], lsend.at[0], lrecv.at[0],
             {"dp": other // chips, "mp": lax.rem(other, chips)},
         )
 
     @pl.when(last)
     def _():
-        lax.fori_loop(1, chips, lambda i, _: (count_copy(i, True).wait_recv(), 0)[1], 0)
+        all_counts().wait_recv()
         totals, where = totals_and_where()
         counts = jnp.sum(count_in[...], axis=0)[0:1, 0:n_mb]
         inverse = 1.0 / jnp.sum(where * counts, axis=1, keepdims=True)
@@ -517,7 +534,7 @@
                 cotp[m, :, cols] = rounded[rank:].astype(F32)[0:1]
         loss_out[...] = jnp.broadcast_to(total, loss_out.shape)
         loss_in[core * chips + place.mp] = loss_out[...]
-        lax.fori_loop(1, 2 * chips, lambda i, _: (loss_copy(i, False).start(), 0)[1], 0)
+        lax.fori_loop(1, 2 * chips, lambda i, _: (loss_copy(i).start(), 0)[1], 0)
         for n in range(width // step):
             cols = pl.ds(n * step, step)
             grads = lax.dot_general(
@@ -531,8 +548,8 @@
     def backward(m, _):
         @pl.when(jnp.logical_not(last))
         def _():
-            for j in range(PIECES):
-                bcopy(m, j).wait_recv()
+            ref = cin.at[m]
+            remote(ref, ref, relayed.at[2], brecv.at[m, 0], {"section": place.prv}).wait_recv()
             bpcopy(m).wait_recv()
 
         for j in range(PIECES):
@@ -550,9 +567,7 @@
         def _():
             for j in range(PIECES):
                 cols = pl.ds(j * tile, tile)
-                back = lax.dot_general(
-                    mix[m], w[cols, :], (((1,), (1,)), ((), ())), preferred_element_type=F32
-                )
+                back = jnp.dot(mix[m], wt[:, cols], preferred_element_type=F32)
                 cout[m, :, cols] = (cin[m, :, cols].astype(F32) + back[:rank]).astype(BF16)
                 cpout[m, :, cols] = (
                     (cpin[m, :, cols] + back[rank : rank + 1]).astype(BF16).astype(F32)
@@ -577,8 +592,8 @@
     def section_copy(step, what):
         other = lax.rem(place.s + step, sections)
         if what == 0:
-            return remote(head_out.at[other], head_land, zsend.at[0, step], zrecv.at[0], {"section": other})
-        return remote(loss_sum, loss_land, zsend.at[1, step], zrecv.at[1], {"section": other})
+            return remote(head_out.at[other], head_land, zsend.at[0], zrecv.at[0], {"section": other})
+        return remote(loss_sum, loss_land, zsend.at[1], zrecv.at[1], {"section": other})
 
     heads = Scatter(place, head_refs, head_sems)
 
@@ -592,8 +607,8 @@
                 head_out[q * (heads.half // per) + k] = value[:, k * per : (k + 1) * per]
 
         heads.run(finish)
-        lax.fori_loop(1, 2 * chips, lambda i, _: (loss_copy(i, True).wait_recv(), 0)[1], 0)
-        loss_sum[...] = jnp.sum(loss_in[...], axis=0)
+        all_losses().wait_recv()
+        loss_sum[...] = jnp.sum(loss_in[...], axis=0) * loss_scale
 
         def spread(i, _):
             section_copy(i, 0).start()
@@ -602,7 +617,7 @@
 
         lax.fori_loop(1, sections, spread, 0)
         o_head[...] = head_out[sections - 1]
-        o_loss[...] = loss_sum[...]
+        o_loss[...] = loss_sum[0:1, 0:1]
 
     sums = Scatter(place, layer_refs, layer_sems)
     sums.products(compact(xin, pin), compact(mix, mixp))
@@ -617,42 +632,35 @@
         section_copy(1, 0).wait_recv()
         section_copy(1, 1).wait_recv()
         o_head[...] = head_land[...]
-        o_loss[...] = loss_land[...]
-
-    def drain(m, _):
-        @pl.when(jnp.logical_not(last))
-        def _():
-            for j in range(PIECES):
-                fcopy(m, j).wait_send()
-            fpcopy(m).wait_send()
-
-        @pl.when(jnp.logical_not(first))
-        def _():
-            for j in range(PIECES):
-                bcopy(m, j).wait_send()
-            bpcopy(m).wait_send()
-
-        return 0
-
-    lax.fori_loop(0, n_mb, drain, 0)
+        o_loss[...] = loss_land[0:1, 0:1]
+
+    def relays_left(ref, n):
+        remote(ref, ref, relayed.at[n], frecv.at[0, 0], {"section": place.nxt}).wait_send()
+
+    @pl.when(jnp.logical_not(last))
+    def _():
+        relays_left(cin, 0)
+        relays_left(pout, 1)
+
+    @pl.when(jnp.logical_not(first))
+    def _():
+        relays_left(cout, 2)
+        relays_left(cpout, 3)
+
     gather.drain()
     sums.drain()
 
     @pl.when(last)
     def _():
         heads.drain()
-        lax.fori_loop(1, chips, lambda i, _: (count_copy(i, False).wait_send(), 0)[1], 0)
-        lax.fori_loop(1, 2 * chips, lambda i, _: (loss_copy(i, False).wait_send(), 0)[1], 0)
-
-        def spread(i, _):
-            section_copy(i, 0).wait_send()
-            section_copy(i, 1).wait_send()
-            return 0
-
-        lax.fori_loop(1, sections, spread, 0)
-
-
-def scatter_scratch(rows, cols):
+        all_counts().wait_send()
+        all_losses().wait_send()
+        for ref, n in ((head_out, 0), (loss_in, 1)):
+            ref = ref.at[pl.ds(0, sections - 1)]
+            remote(ref, ref, zsend.at[n], zrecv.at[n], {"section": place.nxt}).wait_send()
+
+
+def scatter_scratch(rows, cols, depth):
     half = cols // 2
     dma = pltpu.SemaphoreType.DMA
     part = (SIDE, SIDE, rows, cols)
@@ -664,9 +672,8 @@
         pltpu.VMEM((2, 2, SIDE, rows, half), BF16),
         pltpu.VMEM((2, 2, rows // 2, half), BF16),
         pltpu.VMEM((2, 2, rows, half), BF16),
-        dma((SIDE,)), dma((SIDE,)),
-        dma((3, 2, 2)), dma((3, 2, 2)),
-        dma((2, 2, SIDE)), dma((2, 2, SIDE)),
+        pltpu.VMEM((SIDE * rows, depth), BF16),
+        dma((5,)), dma((SIDE,)), dma((3, 2, 2)), dma((2, 2, SIDE)),
     ]
 
 
@@ -682,19 +689,24 @@
     per = out_width // sections
     dma = pltpu.SemaphoreType.DMA
     vmem = pl.BlockSpec(memory_space=pltpu.VMEM)
+    hbm = pl.BlockSpec(memory_space=pl.ANY)
+    like = lambda a: pltpu.VMEM(a.shape, a.dtype)
     row = pltpu.VMEM((n_mb, 1, width), F32)
     block = pltpu.VMEM((n_mb, ROWS, width), BF16)
     send = pltpu.VMEM((n_mb, rank, width), BF16)
     grad_layer, grad_head, loss = pl.pallas_call(
-        functools.partial(step_kernel, sections),
+        functools.partial(step_kernel, sections, 1.0 / (lax.axis_size("dp") * n_mb * out_width)),
         out_shape=(
             jax.ShapeDtypeStruct((own, width), F32),
             jax.ShapeDtypeStruct((own, per), F32),
-            jax.ShapeDtypeStruct((8, 128), F32),
+            jax.ShapeDtypeStruct((1, 1), F32),
         ),
-        in_specs=[vmem] * 9,
+        in_specs=[hbm] * 4 + [vmem] * 2 + [hbm] * 3,
         out_specs=(vmem,) * 3,
         scratch_shapes=[
+            like(inputs), like(tangents), like(targets), like(target_jac), like(encoder),
+            like(layers[0]), like(head_weight),
+            pltpu.VMEM((width, width), BF16),
             pltpu.VMEM((width, width), BF16),
             block, block, block,
             pltpu.VMEM((n_mb, ROWS, out_width), BF16),
@@ -710,15 +722,11 @@
             pltpu.VMEM((8, 128), F32),
             pltpu.VMEM((sections, own, per), F32),
             pltpu.VMEM((own, per), F32),
-            dma((n_mb, PIECES + 1)), dma((n_mb, PIECES + 1)),
-            dma((n_mb, PIECES + 1)), dma((n_mb, PIECES + 1)),
-            dma((2, 4)), dma((2, 4)), dma((2, SIDE, 4)), dma((2, SIDE, 4)),
-            dma((2, 4)), dma((2, 4)), dma((2, SIDE, 4)), dma((2, SIDE, 4)),
-            dma((chips,)), dma((chips,)),
-            dma((2 * chips,)), dma((2 * chips,)),
-            dma((2, sections)), dma((2,)),
-            *scatter_scratch(own, width),
-            *scatter_scratch(own, out_width),
+            dma((7,)), dma((4,)), dma((n_mb, 2)), dma((n_mb, 2)),
+            dma, dma((2, 4)), dma((2, SIDE, 4)), dma, dma,
+            dma((1,)), dma((1,)), dma((1,)), dma((1,)), dma((2,)), dma((2,)),
+            *scatter_scratch(own, width, n_mb * rank + 16),
+            *scatter_scratch(own, out_width, n_mb * rank + 16),
         ],
         compiler_params=pltpu.CompilerParams(
             collective_id=0, has_side_effects=True, vmem_limit_bytes=67043328
@@ -728,8 +736,7 @@
         inputs, tangents, targets, target_jac, rank_mask, batch_order, encoder, layers[0],
         head_weight,
     )
-    loss_value = loss[0, 0] / (lax.axis_size("dp") * n_mb * out_width)
-    return grad_layer[None], grad_head, loss_value
+    return grad_layer[None], grad_head, loss.reshape(())
 
 
 def solution(mesh):

time: 208 us -> 195 us (0.938)
  Pallas kernels: 201 us -> 189 us
    pallas_call x1, Pallas kernels: 201 us -> 189 us  [local(): pl.pallas_call(functools.partial(step_kernel, sections, 1.0 / (lax.axis_s...]
where the time goes in v3:
time: 195 us; the launch traced here: 194 us
  Pallas kernels  189 us (97%)
  local copies, waits for them, and re-layouts  3.25 us (2%)
  between operations  2.38 us (1%)
    pallas_call x1, Pallas kernels, local(): pl.pallas_call(functools.partial(step_kernel, sections, 1.0 / (lax.axis_s...  189 us

profile of v3, /device:TPU:1, one launch (start us, length us, event | category | flops | bytes accessed | tf_op | source)
XLA Modules:
  0.0 194.5 jit_solution(2594209426437341516)
XLA Ops:
  0.6 188.8 %step.1 = (f32[64,2048]{1,0:T(8,128)}, f32[64,128]{1,0:T(8,128)}, f32[1,1]{1,0:T(1,128)}) custom-call(bf16[6,512]{1,0:T(8,128)(2,1)} %refs_0_.1, bf16[6,32,512]{2,1,0:T(8,128)(2,1)} %refs_1_.1, bf16[6,1024]{1,0:T(8,128)(2,1)} %refs_2_.1, bf16[6,32,1024]{2,1,0:T(8,128)(2,1)} %refs_3_.1, s32[6,32]{1,0:T(8,128)} %refs_4_.1, s32[1,6]{1,0:T(1,128)} %refs_5_.1, ...), custom_call_target="tpu_custom_call" | custom-call | tf_op jit(solution)/shard_map/step/pallas_call | solution.py:697
  189.5 1.9 copy.15
  191.3 1.4 copy.16

commit v4 on v3

v4 whole, which is shorter than its diff:
```python
import functools

import jax
import jax.numpy as jnp
from jax import lax
from jax.experimental import pallas as pl
from jax.experimental.pallas import tpu as pltpu
from jax.sharding import PartitionSpec as P

SIDE = 4
ROWS = 48
PIECES = 4
MESH = pl.DeviceIdType.MESH
BF16, F32 = jnp.bfloat16, jnp.float32


def first_row(row, height):
    rows = lax.broadcasted_iota(jnp.int32, (height, row.shape[1]), 0)
    return jnp.where(rows == 0, jnp.broadcast_to(row, (height, row.shape[1])), 0.0)


def stacked_rows(get_row, count, height, width):
    rows = lax.broadcasted_iota(jnp.int32, (height, width), 0)
    block = jnp.zeros((height, width), F32)
    for m in range(count):
        block = jnp.where(rows == m, jnp.broadcast_to(get_row(m), (height, width)), block)
    return block


class Place:
    def __init__(self, sections):
        self.sections = sections
        self.core = lax.axis_index("dp")
        self.s = lax.axis_index("section")
        self.mp = lax.axis_index("mp")
        self.y = self.mp // SIDE
        self.x = lax.rem(self.mp, SIDE)
        self.first = self.s == 0
        self.last = self.s == sections - 1
        self.nxt = lax.rem(self.s + 1, sections)
        self.prv = lax.rem(self.s + sections - 1, sections)

    def along(self, coordinate, steps):
        return lax.rem(coordinate + steps + SIDE, SIDE)

    def chip(self, axis, steps):
        if axis == 0:
            return self.y * SIDE + self.along(self.x, steps)
        return self.along(self.y, steps) * SIDE + self.x


def remote(src, dst, send, recv, device_id):
    return pltpu.make_async_remote_copy(
        src_ref=src, dst_ref=dst, send_sem=send, recv_sem=recv,
        device_id=device_id, device_id_type=MESH,
    )


def neighbours(place):
    for axis in (0, 1):
        for steps in (1, -1):
            yield {"mp": place.chip(axis, steps)}
    yield {"dp": 1 - place.core}
    yield {"section": place.nxt}
    yield {"section": place.prv}


def knock(place):
    barrier = pltpu.get_barrier_semaphore()
    for device in neighbours(place):
        pl.semaphore_signal(barrier, inc=1, device_id=device, device_id_type=MESH)


def enter():
    pl.semaphore_wait(pltpu.get_barrier_semaphore(), 7)


class Gather:
    def __init__(self, place, shard, w, sems):
        self.p, self.shard, self.w = place, shard, w
        self.sent, self.recv1, self.recv2, self.dsent, self.dgot = sems
        self.depth = shard.shape[0]
        self.piece = self.depth // 4

    def rows(self, q, core, step1, step2, half):
        p = self.p
        dx, dy = (step1, step2) if q == 0 else (step2, step1)
        chip = p.along(p.y, dy) * SIDE + p.along(p.x, dx)
        start = chip * self.depth + core * (2 * self.piece) + q * self.piece
        length = self.piece
        if half is not None:
            length = self.piece // 2
            start = start + half * length
        return pl.ds(pl.multiple_of(start, length), length)

    def copy(self, q, phase, o, e):
        p = self.p
        axis = q if phase == 1 else 1 - q
        to = 1 if e in (0, 2) else -1
        back = {0: 0, 1: 0, 2: -1, 3: 1}[e]
        half = {0: None, 1: None, 2: 0, 3: 1}[e]
        step1, step2 = (back, 0) if phase == 1 else (o, back)
        dst = self.w.at[self.rows(q, p.core, step1, step2, half)]
        src = dst
        if step1 == 0 and step2 == 0:
            src = self.shard.at[pl.ds(pl.multiple_of(p.core * (2 * self.piece) + q * self.piece, self.piece), self.piece)]
        return remote(src, dst, self.sent, self.recv(phase, q, o, e), {"mp": p.chip(axis, to)})

    def recv(self, phase, q, o, e):
        return self.recv1.at[q, e] if phase == 1 else self.recv2.at[q, o % SIDE, e]

    def arrived(self, q, phase, o, e):
        p = self.p
        away = {0: -1, 1: 1, 2: -2, 3: 2}[e]
        half = {0: None, 1: None, 2: 0, 3: 1}[e]
        step1, step2 = (away, 0) if phase == 1 else (o, away)
        return self.p, q, step1, step2, half

    def wait(self, q, phase, o, e):
        p, q, step1, step2, half = self.arrived(q, phase, o, e)
        dst = self.w.at[self.rows(q, p.core, step1, step2, half)]
        remote(dst, dst, self.sent, self.recv(phase, q, o, e), {"mp": p.chip(0, 1)}).wait_recv()
        remote(dst, dst, self.dsent, self.dgot, {"dp": 1 - p.core}).start()

    def all_of(self, send, recv):
        ref = self.w.at[pl.ds(0, (SIDE * SIDE - 1) * 2 * self.piece)]
        return remote(ref, ref, send, recv, {"dp": 1 - self.p.core})

    def begin(self):
        for q in (0, 1):
            self.copy(q, 1, 0, 0).start()
            self.copy(q, 1, 0, 1).start()
        for q in (0, 1):
            self.copy(q, 2, 0, 0).start()
            self.copy(q, 2, 0, 1).start()
        p = self.p
        self.w[pl.ds(pl.multiple_of(p.mp * self.depth, self.depth), self.depth), :] = self.shard[...]

    def run(self):
        for q in (0, 1):
            self.wait(q, 1, 0, 0)
            self.copy(q, 1, 0, 2).start()
            self.wait(q, 1, 0, 1)
            self.copy(q, 1, 0, 3).start()
        for q in (0, 1):
            for o in (-1, 1):
                self.copy(q, 2, o, 0).start()
                self.copy(q, 2, o, 1).start()
        for q in (0, 1):
            self.wait(q, 2, 0, 0)
            self.copy(q, 2, 0, 2).start()
            self.wait(q, 2, 0, 1)
            self.copy(q, 2, 0, 3).start()
        for q in (0, 1):
            self.wait(q, 1, 0, 2)
            self.wait(q, 1, 0, 3)
            self.copy(q, 2, 2, 0).start()
            self.copy(q, 2, 2, 1).start()
        for o in (-1, 1, 2):
            for q in (0, 1):
                self.wait(q, 2, o, 0)
                self.copy(q, 2, o, 2).start()
                self.wait(q, 2, o, 1)
                self.copy(q, 2, o, 3).start()
        for o in (0, -1, 1, 2):
            for q in (0, 1):
                self.wait(q, 2, o, 2)
                self.wait(q, 2, o, 3)
        self.all_of(self.dsent, self.dgot).wait_recv()

    def drain(self):
        self.all_of(self.sent, self.dgot).wait_send()
        self.all_of(self.dsent, self.dgot).wait_send()


class Scatter:
    STEPS = (2, 1, -1, 0)

    def __init__(self, place, refs, sems):
        self.p = place
        self.gs, self.gd, self.g, self.l1, self.l2, self.l3, self.l4, self.turned, self.right = refs
        self.sent, self.drecv, self.recv, self.recv2 = sems
        self.half = self.g.shape[3] // 2

    def cols(self, q):
        return pl.ds(q * self.half, self.half)

    def order(self, q):
        p = self.p
        return [p.along(p.x if q == 0 else p.y, steps) for steps in self.STEPS]

    def block(self, q, first, second):
        return (first, second) if q == 0 else (second, first)

    def ring1(self, q, steps):
        p = self.p
        return p.along(p.y if q == 0 else p.x, steps)

    def group(self, q, k):
        at = self.ring1(q, self.STEPS[k])
        return (at, slice(None)) if q == 0 else (slice(None), at)

    def pair(self, q, first, low):
        if q == 0:
            return self.g.at[first, pl.ds(low, 2), :, self.cols(q)]
        return self.g.at[pl.ds(low, 2), first, :, self.cols(q)]

    def copy1(self, q, d):
        src = self.pair(q, self.ring1(q, 2), 2 * d)
        return remote(src, self.l1.at[q, d], self.sent.at[1], self.recv.at[0, q, d],
                      {"mp": self.p.chip(1 - q, 1 if d == 0 else -1)})

    def copy2(self, q, d, k):
        to = 1 if d == 0 else -1
        a, b = self.block(q, self.ring1(q, to), self.order(q)[k])
        return remote(self.g.at[a, b, :, self.cols(q)], self.l2.at[q, d, k],
                      self.sent.at[2], self.recv2.at[q, d, k], {"mp": self.p.chip(1 - q, to)})

    def copy3(self, q, d):
        a, b = self.block(q, self.ring1(q, 0), self.order(q)[0])
        n = self.g.shape[2] // 2
        return remote(self.g.at[a, b, pl.ds(d * n, n), self.cols(q)], self.l3.at[q, d],
                      self.sent.at[3], self.recv.at[1, q, d],
                      {"mp": self.p.chip(q, 1 if d == 0 else -1)})

    def copy4(self, q, d):
        a, b = self.block(q, self.ring1(q, 0), self.order(q)[1 + d])
        return remote(self.g.at[a, b, :, self.cols(q)], self.l4.at[q, d],
                      self.sent.at[4], self.recv.at[2, q, d],
                      {"mp": self.p.chip(q, 1 if d == 0 else -1)})

    def exchange(self, q, k):
        index = (*self.group(q, k), slice(None), self.cols(q))
        return remote(self.gs.at[index], self.gd.at[index], self.sent.at[0], self.drecv.at[q, k],
                      {"dp": 1 - self.p.core})

    def turn(self, left):
        per = self.g.shape[1] * self.g.shape[2]

        def one(n, _):
            block = left(pl.ds(pl.multiple_of(n * per, per), per)).T
            self.turned[n // SIDE, lax.rem(n, SIDE)] = block.reshape(SIDE, self.g.shape[2], block.shape[1])
            return 0

        lax.fori_loop(0, 2 * SIDE, one, 0)

    def product(self, core, q, k):
        rows = self.turned[(core, *self.group(q, k))]
        rows = rows.reshape(-1, rows.shape[2])
        value = jnp.dot(rows, self.right[:, self.cols(q)], preferred_element_type=F32)
        return value.reshape(SIDE, self.g.shape[2], self.half)

    def other(self, q, k):
        index = (*self.group(q, k), slice(None), self.cols(q))
        self.gs[index] = self.product(1 - self.p.core, q, k).astype(BF16)
        self.exchange(q, k).start()

    def own(self, q, k):
        index = (*self.group(q, k), slice(None), self.cols(q))
        value = self.product(self.p.core, q, k)
        self.exchange(q, k).wait_recv()
        self.g[index] = (value + self.gd[index].astype(F32)).astype(BF16)
        if k == 0:
            self.copy1(q, 0).start()
            self.copy1(q, 1).start()

    def products(self):
        parts = [(q, k) for k in range(SIDE) for q in (0, 1)]
        ahead = 3
        for n in range(len(parts) + ahead):
            if n < len(parts):
                self.other(*parts[n])
            if n >= ahead:
                self.own(*parts[n - ahead])

    def add(self, index, value):
        self.g[index] = (self.g[index].astype(F32) + value.astype(F32)).astype(BF16)

    def arrived(self, q, k):
        self.copy2(q, 0, k).wait_recv()
        self.copy2(q, 1, k).wait_recv()
        return self.l2[q, 0, k].astype(F32) + self.l2[q, 1, k].astype(F32)

    def run(self, finish):
        n = self.g.shape[2] // 2
        index = lambda q, k: (*self.block(q, self.ring1(q, 0), self.order(q)[k]), slice(None), self.cols(q))
        for d in (0, 1):
            for q in (0, 1):
                self.copy1(q, d).wait_recv()
                first = self.ring1(q, 1 if d == 0 else -1)
                for k in (0, 1):
                    a, b = self.block(q, first, 2 * d + k)
                    self.add((a, b, slice(None), self.cols(q)), self.l1[q, d, k])
                self.copy2(q, d, 0).start()
                self.copy2(q, d, 1).start()
        for q in (0, 1):
            self.add(index(q, 0), self.arrived(q, 0))
            self.copy3(q, 0).start()
            self.copy3(q, 1).start()
            for k in (2, 3):
                self.copy2(q, 0, k).start()
                self.copy2(q, 1, k).start()
        for d in (0, 1):
            for q in (0, 1):
                self.add(index(q, 1 + d), self.arrived(q, 1 + d))
                a, b, _, cols = index(q, 1 + d)
                self.copy3(q, d).wait_recv()
                self.add((a, b, pl.ds(d * n, n), cols), self.l3[q, d])
                self.copy4(q, d).start()
        for q in (0, 1):
            value = self.g[index(q, 3)].astype(F32) + self.arrived(q, 3)
            self.copy4(q, 0).wait_recv()
            self.copy4(q, 1).wait_recv()
            finish(q, value + self.l4[q, 0].astype(F32) + self.l4[q, 1].astype(F32))

    def drain(self):
        for n, ref in enumerate((self.gd, self.l1, self.l2, self.l3, self.l4)):
            remote(ref, ref, self.sent.at[n], self.drecv.at[0, 0], {"dp": 1 - self.p.core}).wait_send()


def step_kernel(sections, loss_scale, *refs):
    (
        h_inputs, h_tangents, h_targets, h_target_jac, mask, batch_order, h_encoder, h_shard, h_head,
        o_layer, o_head, o_loss,
        inputs, tangents, targets, target_jac, shard, head,
        w, wt, head_t, xin, xout, mix, cot, pin, pout, pre, thb, cin, cpin, cout, cpout, mixp, cotp,
        o_layer_buf, coef, wantp, count_out, count_in, loss_out, loss_in, loss_sum, loss_land, head_out, head_land,
        loads, stored, relayed, frecv, brecv,
        gsent, grecv1, grecv2, dsent, dgot,
        csend, crecv, lsend, lrecv, zsend, zrecv,
        *scatter,
    ) = refs
    layer_refs, layer_sems = scatter[:9], scatter[9:13]
    head_refs, head_sems = scatter[13:22], scatter[22:26]
    n_mb, rows, width = xin.shape
    rank = cin.shape[1]
    out_width = head.shape[1]
    tile = width // PIECES
    place = Place(sections)
    s, core, first, last = place.s, place.core, place.first, place.last
    chips = SIDE * SIDE

    encoder = head_t.at[pl.ds(0, h_encoder.shape[0])]

    def load(n):
        pairs = (
            (h_shard, shard), (h_inputs, inputs), (h_tangents, tangents), (h_encoder, encoder),
            (h_targets, targets), (h_target_jac, target_jac), (h_head, head),
        )
        return pltpu.make_async_copy(pairs[n][0], pairs[n][1], loads.at[n])

    for n in range(7):
        load(n).start()
    knock(place)

    @pl.when(first)
    def _():
        for n in (1, 2, 3):
            load(n).wait()
        primal = inputs[...].astype(F32)
        for m in range(n_mb):
            lhs = jnp.concatenate(
                [tangents[m], first_row(primal[m : m + 1], rows - rank).astype(BF16)], axis=0
            )
            lifted = jnp.dot(lhs, encoder[...], preferred_element_type=F32).astype(BF16)
            xin[m] = lifted
            pin[m] = lifted[rank:].astype(F32)[0:1]

    load(0).wait()
    enter()
    gather = Gather(place, shard, w, (gsent, grecv1, grecv2, dsent, dgot))
    gather.begin()
    gather.run()
    for n in (4, 5, 6):
        load(n).wait()

    @pl.when(jnp.logical_not(first))
    def _():
        for n in (1, 2, 3):
            load(n).wait()

    def count_copy(step):
        other = lax.rem(place.mp + step, chips)
        return remote(count_out, count_in.at[place.mp], csend.at[0], crecv.at[0], {"mp": other})

    def all_counts():
        ref = count_in.at[pl.ds(0, chips - 1)]
        return remote(ref, ref, csend.at[0], crecv.at[0], {"dp": 1 - core})

    def all_losses():
        ref = loss_in.at[pl.ds(0, 2 * chips - 1)]
        return remote(ref, ref, lsend.at[0], lrecv.at[0], {"dp": 1 - core})

    def turned_into(target, source):
        high, wide = source.shape
        step = 512 if high % 512 == 0 and wide % 512 == 0 else min(high, wide)
        count = wide // step

        def turn(n, _):
            a = pl.ds(pl.multiple_of((n // count) * step, step), step)
            b = pl.ds(pl.multiple_of(lax.rem(n, count) * step, step), step)
            target[b, a] = source[a, b].T
            return 0

        lax.fori_loop(0, (high // step) * count, turn, 0)

    @pl.when(last)
    def _():
        totals = 1.0 + jnp.sum(mask[...].astype(F32), axis=1, keepdims=True)
        where = lax.broadcasted_iota(jnp.int32, (n_mb, n_mb), 0) == jnp.broadcast_to(
            batch_order[...], (n_mb, n_mb)
        )
        where = where.astype(F32)
        count_out[...] = jnp.zeros_like(count_out)
        count_out[0:1, 0:n_mb] = jnp.sum(where * totals, axis=0, keepdims=True)
        count_in[place.mp] = count_out[...]
        lax.fori_loop(1, chips, lambda i, _: (count_copy(i).start(), 0)[1], 0)
        turned_into(head_t, head)
        all_counts().wait_recv()
        counts = jnp.sum(count_in[...], axis=0)[0:1, 0:n_mb]
        inverse = 1.0 / jnp.sum(where * counts, axis=1, keepdims=True)
        row = lax.broadcasted_iota(jnp.int32, (rows, 1), 0)
        ranks = totals.astype(jnp.int32) - 1
        primal_wanted = targets[...].astype(F32)
        for m in range(n_mb):
            present = jnp.logical_or(row < ranks[m : m + 1], row == rank)
            coef[m] = jnp.where(present, inverse[m : m + 1], 0.0)
            wantp[m] = primal_wanted[m : m + 1]
        loss_out[...] = jnp.zeros_like(loss_out)

    late = s >= sections // 2

    @pl.when(late)
    def _():
        turned_into(wt, w)

    def fcopy(m, j):
        cols = pl.ds(j * tile, tile)
        return remote(
            xout.at[m, pl.ds(0, rank), cols], xin.at[m, pl.ds(0, rank), cols],
            relayed.at[0], frecv.at[m, 0], {"section": place.nxt},
        )

    def fpcopy(m):
        return remote(
            pout.at[m], pin.at[m], relayed.at[1], frecv.at[m, 1], {"section": place.nxt}
        )

    def bcopy(m, j):
        cols = pl.ds(j * tile, tile)
        return remote(
            cout.at[m, :, cols], cin.at[m, :, cols],
            relayed.at[2], brecv.at[m, 0], {"section": place.prv},
        )

    def bpcopy(m):
        return remote(
            cpout.at[m], cpin.at[m], relayed.at[3], brecv.at[m, 1], {"section": place.prv}
        )

    def forward(m, span, sending):
        @pl.when(jnp.logical_not(first))
        def _():
            for i in range(span):
                ref = xin.at[m + i, pl.ds(0, rank)]
                remote(ref, ref, relayed.at[0], frecv.at[m + i, 0], {"section": place.nxt}).wait_recv()
                fpcopy(m + i).wait_recv()
                xin[m + i, pl.ds(rank, rows - rank), :] = first_row(pin[m + i], rows - rank).astype(BF16)

        for j in range(PIECES):
            cols = pl.ds(j * tile, tile)
            both = jnp.dot(
                xin[pl.ds(m, span)].reshape(span * rows, width), w[:, cols], preferred_element_type=F32
            )
            for i in range(span):
                acc = both[i * rows : i * rows + rows]
                th = jnp.tanh(acc[rank : rank + 1, :])
                slope = 1.0 - th * th
                tangent = acc[:rank, :]
                pre[m + i, :, cols] = tangent
                thb[m + i, :, cols] = th
                moved = xin[m + i, pl.ds(0, rank), cols].astype(F32) + slope * tangent
                xout[m + i, pl.ds(0, rank), cols] = moved.astype(BF16)
                primal = (pin[m + i, :, cols] + th).astype(BF16).astype(F32)
                pout[m + i, :, cols] = primal
                xout[m + i, pl.ds(rank, rows - rank), cols] = first_row(primal, rows - rank).astype(BF16)
                if sending:
                    fcopy(m + i, j).start()
        if sending:
            for i in range(span):
                fpcopy(m + i).start()

    def loss_copy(step):
        plane = 2 * chips
        me = core * chips + place.mp
        other = lax.rem(me + step, plane)
        return remote(
            loss_out, loss_in.at[me], lsend.at[0], lrecv.at[0],
            {"dp": other // chips, "mp": lax.rem(other, chips)},
        )

    def objective(m, span):
        step = min(256, out_width)
        total = jnp.zeros((1, 1), F32)
        for n in range(out_width // step):
            cols = pl.ds(n * step, step)
            outputs = jnp.dot(
                xout[pl.ds(m, span)].reshape(span * rows, width), head[:, cols],
                preferred_element_type=F32,
            )
            for i in range(span):
                wanted = jnp.concatenate(
                    [
                        target_jac[m + i, :, cols].astype(F32),
                        first_row(wantp[m + i, :, cols], rows - rank),
                    ],
                    axis=0,
                )
                mismatch = outputs[i * rows : (i + 1) * rows] - wanted
                weighted = coef[m + i] * mismatch
                total = total + jnp.sum(
                    jnp.sum(weighted * mismatch, axis=0, keepdims=True), axis=1, keepdims=True
                )
                rounded = (2.0 * weighted).astype(BF16)
                cot[m + i, :, cols] = rounded
                cotp[m + i, :, cols] = rounded[rank:].astype(F32)[0:1]
        loss_out[...] = loss_out[...] + jnp.broadcast_to(total, loss_out.shape)
        for j in range(PIECES):
            cols = pl.ds(j * tile, tile)
            grads = jnp.dot(
                cot[pl.ds(m, span)].reshape(span * rows, out_width), head_t[:, cols],
                preferred_element_type=F32,
            ).astype(BF16)
            for i in range(span):
                cin[m + i, :, cols] = grads[i * rows : i * rows + rank, :]
                cpin[m + i, :, cols] = grads[i * rows + rank : (i + 1) * rows, :].astype(F32)[0:1]

    def mixed(m):
        for j in range(PIECES):
            cols = pl.ds(j * tile, tile)
            upstream = cin[m, :, cols].astype(F32)
            th = thb[m, :, cols]
            slope = 1.0 - th * th
            mix[m, pl.ds(0, rank), cols] = (upstream * slope).astype(BF16)
            total = jnp.sum(upstream * pre[m, :, cols], axis=0, keepdims=True)
            primal = cpin[m, :, cols] * slope - 2.0 * total * th * slope
            mixp[m, :, cols] = primal
            mix[m, pl.ds(rank, rows - rank), cols] = first_row(primal, rows - rank).astype(BF16)

    def backward(m, span):
        for i in range(span):
            mixed(m + i)

        @pl.when(jnp.logical_not(first))
        def _():
            for j in range(PIECES):
                cols = pl.ds(j * tile, tile)
                both = jnp.dot(
                    mix[pl.ds(m, span)].reshape(span * rows, width), wt[:, cols],
                    preferred_element_type=F32,
                )
                for i in range(span):
                    back = both[i * rows : (i + 1) * rows]
                    cout[m + i, :, cols] = (cin[m + i, :, cols].astype(F32) + back[:rank]).astype(BF16)
                    cpout[m + i, :, cols] = (
                        (cpin[m + i, :, cols] + back[rank : rank + 1]).astype(BF16).astype(F32)
                    )
                bcopy(m, j).start()
            bpcopy(m).start()
            for i in range(1, span):
                for j in range(PIECES):
                    bcopy(m + i, j).start()
                bpcopy(m + i).start()

    heads = Scatter(place, head_refs, head_sems)
    sums = Scatter(place, layer_refs, layer_sems)

    def compact(tangent, primal):
        def take(cols):
            block = tangent[:, pl.ds(0, rank), cols]
            rest = stacked_rows(lambda m: primal[m, :, cols], n_mb, 16, block.shape[2])
            return jnp.concatenate(
                [block.reshape(n_mb * rank, block.shape[2]), rest.astype(BF16)], axis=0
            )

        return take

    @pl.when(last)
    def _():
        span = 2

        def group(g, _):
            forward(g * span, span, False)
            objective(g * span, span)
            backward(g * span, span)
            return 0

        lax.fori_loop(0, n_mb // span, group, 0)
        loss_in[core * chips + place.mp] = loss_out[...]
        lax.fori_loop(1, 2 * chips, lambda i, _: (loss_copy(i).start(), 0)[1], 0)
        sums.turn(compact(xin, pin))

    @pl.when(jnp.logical_not(last))
    def _():
        lax.fori_loop(0, n_mb, lambda m, _: (forward(m, 1, True), 0)[1], 0)

        @pl.when(jnp.logical_not(jnp.logical_or(late, first)))
        def _():
            turned_into(wt, w)

        sums.turn(compact(xin, pin))

        def back(m, _):
            ref = cin.at[m]
            remote(ref, ref, relayed.at[2], brecv.at[m, 0], {"section": place.prv}).wait_recv()
            bpcopy(m).wait_recv()
            backward(m, 1)
            return 0

        lax.fori_loop(0, n_mb, back, 0)

    def section_copy(step, what):
        other = lax.rem(place.s + step, sections)
        if what == 0:
            return remote(head_out.at[other], head_land, zsend.at[0], zrecv.at[0], {"section": other})
        return remote(loss_sum, loss_land, zsend.at[1], zrecv.at[1], {"section": other})

    @pl.when(last)
    def _():
        heads.turn(compact(xout, pout))
        heads.right[...] = compact(cot, cotp)(slice(None))
        heads.products()

        def finish(q, value):
            per = out_width // sections
            for k in range(heads.half // per):
                head_out[q * (heads.half // per) + k] = value[:, k * per : (k + 1) * per]

        heads.run(finish)
        all_losses().wait_recv()
        loss_sum[...] = jnp.sum(loss_in[...], axis=0) * loss_scale

        def spread(i, _):
            section_copy(i, 0).start()
            section_copy(i, 1).start()
            return 0

        lax.fori_loop(1, sections, spread, 0)
        o_head[...] = head_out[sections - 1]
        o_loss[...] = loss_sum[0:1, 0:1]

    sums.right[...] = compact(mix, mixp)(slice(None))
    sums.products()

    def layer_out(q):
        cols = pl.ds(q * sums.half, sums.half)
        return pltpu.make_async_copy(o_layer_buf.at[:, cols], o_layer.at[:, cols], stored.at[q])

    def finish_layer(q, value):
        o_layer_buf[:, pl.ds(q * sums.half, sums.half)] = value
        layer_out(q).start()

    sums.run(finish_layer)

    @pl.when(jnp.logical_not(last))
    def _():
        section_copy(1, 0).wait_recv()
        section_copy(1, 1).wait_recv()
        o_head[...] = head_land[...]
        o_loss[...] = loss_land[0:1, 0:1]

    def relays_left(ref, n):
        remote(ref, ref, relayed.at[n], frecv.at[0, 0], {"section": place.nxt}).wait_send()

    @pl.when(jnp.logical_not(last))
    def _():
        relays_left(cin, 0)
        relays_left(pout, 1)

    @pl.when(jnp.logical_not(first))
    def _():
        relays_left(cout, 2)
        relays_left(cpout, 3)

    gather.drain()
    sums.drain()
    layer_out(0).wait()
    layer_out(1).wait()

    @pl.when(last)
    def _():
        heads.drain()
        all_counts().wait_send()
        all_losses().wait_send()
        for ref, n in ((head_out, 0), (loss_in, 1)):
            ref = ref.at[pl.ds(0, sections - 1)]
            remote(ref, ref, zsend.at[n], zrecv.at[n], {"section": place.nxt}).wait_send()


def scatter_scratch(rows, cols, depth):
    half = cols // 2
    dma = pltpu.SemaphoreType.DMA
    part = (SIDE, SIDE, rows, cols)
    return [
        pltpu.VMEM(part, BF16),
        pltpu.VMEM(part, BF16),
        pltpu.VMEM(part, BF16),
        pltpu.VMEM((2, 2, 2, rows, half), BF16),
        pltpu.VMEM((2, 2, SIDE, rows, half), BF16),
        pltpu.VMEM((2, 2, rows // 2, half), BF16),
        pltpu.VMEM((2, 2, rows, half), BF16),
        pltpu.VMEM((2, SIDE, SIDE, rows, depth), BF16),
        pltpu.VMEM((depth, cols), BF16),
        dma((5,)), dma((2, SIDE)), dma((3, 2, 2)), dma((2, 2, SIDE)),
    ]


def local(
    inputs, tangents, targets, target_jac, rank_mask, batch_order, encoder, layers, head_weight
):
    n_mb, rank, _ = tangents.shape
    width = layers.shape[2]
    out_width = head_weight.shape[1]
    sections = lax.axis_size("section")
    chips = SIDE * SIDE
    own = width // (2 * chips)
    per = out_width // sections
    dma = pltpu.SemaphoreType.DMA
    vmem = pl.BlockSpec(memory_space=pltpu.VMEM)
    hbm = pl.BlockSpec(memory_space=pl.ANY)
    like = lambda a: pltpu.VMEM(a.shape, a.dtype)
    row = pltpu.VMEM((n_mb, 1, width), F32)
    block = pltpu.VMEM((n_mb, ROWS, width), BF16)
    send = pltpu.VMEM((n_mb, rank, width), BF16)
    grad_layer, grad_head, loss = pl.pallas_call(
        functools.partial(step_kernel, sections, 1.0 / (lax.axis_size("dp") * n_mb * out_width)),
        out_shape=(
            jax.ShapeDtypeStruct((own, width), F32),
            jax.ShapeDtypeStruct((own, per), F32),
            jax.ShapeDtypeStruct((1, 1), F32),
        ),
        in_specs=[hbm] * 4 + [vmem] * 2 + [hbm] * 3,
        out_specs=(hbm, vmem, vmem),
        scratch_shapes=[
            like(inputs), like(tangents), like(targets), like(target_jac),
            like(layers[0]), like(head_weight),
            pltpu.VMEM((width, width), BF16),
            pltpu.VMEM((width, width), BF16),
            pltpu.VMEM((out_width, width), BF16),
            block, block, block,
            pltpu.VMEM((n_mb, ROWS, out_width), BF16),
            row, row,
            pltpu.VMEM((n_mb, rank, width), F32),
            row, send, row, send, row, row,
            pltpu.VMEM((n_mb, 1, out_width), F32),
            pltpu.VMEM((own, width), F32),
            pltpu.VMEM((n_mb, ROWS, 1), F32),
            pltpu.VMEM((n_mb, 1, out_width), F32),
            pltpu.VMEM((8, 128), F32),
            pltpu.VMEM((chips, 8, 128), F32),
            pltpu.VMEM((8, 128), F32),
            pltpu.VMEM((2 * chips, 8, 128), F32),
            pltpu.VMEM((8, 128), F32),
            pltpu.VMEM((8, 128), F32),
            pltpu.VMEM((sections, own, per), F32),
            pltpu.VMEM((own, per), F32),
            dma((7,)), dma((2,)), dma((4,)), dma((n_mb, 2)), dma((n_mb, 2)),
            dma, dma((2, 4)), dma((2, SIDE, 4)), dma, dma,
            dma((1,)), dma((1,)), dma((1,)), dma((1,)), dma((2,)), dma((2,)),
            *scatter_scratch(own, width, n_mb * rank + 16),
            *scatter_scratch(own, out_width, n_mb * rank + 16),
        ],
        compiler_params=pltpu.CompilerParams(
            collective_id=0, has_side_effects=True, vmem_limit_bytes=67043328
        ),
        name="step",
    )(
        inputs, tangents, targets, target_jac, rank_mask, batch_order, encoder, layers[0],
        head_weight,
    )
    return grad_layer[None], grad_head, loss.reshape(())


def solution(mesh):
    in_specs = (
        P(("dp", "mp"), None),
        P(("dp", "mp"), None, None),
        P(("dp", "mp"), None),
        P(("dp", "mp"), None, None),
        P(("dp", "mp"), None),
        P(("dp", "mp"), None),
        P(),
        P("section", "mp", None),
        P(),
    )
    out_specs = (P("section", ("dp", "mp"), None), P(("dp", "mp"), "section"), P())
    return jax.shard_map(local, mesh=mesh, in_specs=in_specs, out_specs=out_specs, check_vma=False)
```

time: 195 us -> 172 us (0.88)
  Pallas kernels: 189 us -> 166 us
    pallas_call x1, Pallas kernels: 189 us -> 166 us  [local(): pl.pallas_call(functools.partial(step_kernel, sections, 1.0 / (lax.axis_s...]
where the time goes in v4:
time: 172 us
  Pallas kernels  166 us (97%)
  local copies, waits for them, and re-layouts  3.25 us (2%)
  between operations  2.38 us (1%)
    pallas_call x1, Pallas kernels, local(): pl.pallas_call(functools.partial(step_kernel, sections, 1.0 / (lax.axis_s...  166 us

profile of v4, /device:TPU:1, one launch (start us, length us, event | category | flops | bytes accessed | tf_op | source)
XLA Modules:
  0.0 172.0 jit_solution(8275700879217627342)
XLA Ops:
  0.6 166.4 %step.1 = (f32[64,2048]{1,0:T(8,128)}, f32[64,128]{1,0:T(8,128)}, f32[1,1]{1,0:T(1,128)}) custom-call(bf16[6,512]{1,0:T(8,128)(2,1)} %refs_0_.1, bf16[6,32,512]{2,1,0:T(8,128)(2,1)} %refs_1_.1, bf16[6,1024]{1,0:T(8,128)(2,1)} %refs_2_.1, bf16[6,32,1024]{2,1,0:T(8,128)(2,1)} %refs_3_.1, s32[6,32]{1,0:T(8,128)} %refs_4_.1, s32[1,6]{1,0:T(1,128)} %refs_5_.1, ...), custom_call_target="tpu_custom_call" | custom-call | tf_op jit(solution)/shard_map/step/pallas_call | solution.py:735
  167.0 1.9 %copy.15 = f32[1,64,2048]{2,1,0:T(8,128)} copy(f32[1,64,2048]{2,1,0:T(8,128)} %bitcast.4) | data formatting | bytes 1048576
  168.9 1.4 copy.16

commit v5 on v4

--- a/solution.py
+++ b/solution.py
@@ -9,7 +9,7 @@
 
 SIDE = 4
 ROWS = 48
-PIECES = 4
+PIECES = 2
 MESH = pl.DeviceIdType.MESH
 BF16, F32 = jnp.bfloat16, jnp.float32
 
@@ -37,6 +37,8 @@
         self.x = lax.rem(self.mp, SIDE)
         self.first = self.s == 0
         self.last = self.s == sections - 1
+        self.middle = jnp.logical_not(jnp.logical_or(self.first, self.last))
+        self.carrier = jnp.logical_and(self.middle, self.core == 1)
         self.nxt = lax.rem(self.s + 1, sections)
         self.prv = lax.rem(self.s + sections - 1, sections)
 
@@ -61,8 +63,9 @@
         for steps in (1, -1):
             yield {"mp": place.chip(axis, steps)}
     yield {"dp": 1 - place.core}
-    yield {"section": place.nxt}
-    yield {"section": place.prv}
+    for section in (place.nxt, place.prv):
+        for core in (0, 1):
+            yield {"dp": core, "section": section}
 
 
 def knock(place):
@@ -72,7 +75,7 @@
 
 
 def enter():
-    pl.semaphore_wait(pltpu.get_barrier_semaphore(), 7)
+    pl.semaphore_wait(pltpu.get_barrier_semaphore(), 9)
 
 
 class Gather:
@@ -179,7 +182,7 @@
     def __init__(self, place, refs, sems):
         self.p = place
         self.gs, self.gd, self.g, self.l1, self.l2, self.l3, self.l4, self.turned, self.right = refs
-        self.sent, self.drecv, self.recv, self.recv2 = sems
+        self.sent, self.drecv, self.recv, self.recv2, self.recv4 = sems
         self.half = self.g.shape[3] // 2
 
     def cols(self, q):
@@ -210,11 +213,11 @@
         return remote(src, self.l1.at[q, d], self.sent.at[1], self.recv.at[0, q, d],
                       {"mp": self.p.chip(1 - q, 1 if d == 0 else -1)})
 
-    def copy2(self, q, d, k):
+    def copy2(self, q, d, b):
         to = 1 if d == 0 else -1
-        a, b = self.block(q, self.ring1(q, to), self.order(q)[k])
-        return remote(self.g.at[a, b, :, self.cols(q)], self.l2.at[q, d, k],
-                      self.sent.at[2], self.recv2.at[q, d, k], {"mp": self.p.chip(1 - q, to)})
+        at = self.block(q, self.ring1(q, to), b)
+        return remote(self.g.at[(*at, slice(None), self.cols(q))], self.l2.at[q, d, b],
+                      self.sent.at[2], self.recv2.at[q, d, b], {"mp": self.p.chip(1 - q, to)})
 
     def copy3(self, q, d):
         a, b = self.block(q, self.ring1(q, 0), self.order(q)[0])
@@ -223,10 +226,12 @@
                       self.sent.at[3], self.recv.at[1, q, d],
                       {"mp": self.p.chip(q, 1 if d == 0 else -1)})
 
-    def copy4(self, q, d):
+    def copy4(self, q, d, h):
         a, b = self.block(q, self.ring1(q, 0), self.order(q)[1 + d])
-        return remote(self.g.at[a, b, :, self.cols(q)], self.l4.at[q, d],
-                      self.sent.at[4], self.recv.at[2, q, d],
+        n = self.g.shape[2] // 2
+        rows = pl.ds(h * n, n)
+        return remote(self.g.at[a, b, rows, self.cols(q)], self.l4.at[q, d, rows],
+                      self.sent.at[4], self.recv4.at[q, d, h],
                       {"mp": self.p.chip(q, 1 if d == 0 else -1)})
 
     def exchange(self, q, k):
@@ -263,6 +268,10 @@
         if k == 0:
             self.copy1(q, 0).start()
             self.copy1(q, 1).start()
+        elif k < 3:
+            d = k - 1
+            self.copy2(q, d, 2 - 2 * d).start()
+            self.copy2(q, d, 3 - 2 * d).start()
 
     def products(self):
         parts = [(q, k) for k in range(SIDE) for q in (0, 1)]
@@ -277,9 +286,10 @@
         self.g[index] = (self.g[index].astype(F32) + value.astype(F32)).astype(BF16)
 
     def arrived(self, q, k):
-        self.copy2(q, 0, k).wait_recv()
-        self.copy2(q, 1, k).wait_recv()
-        return self.l2[q, 0, k].astype(F32) + self.l2[q, 1, k].astype(F32)
+        b = self.order(q)[k]
+        self.copy2(q, 0, b).wait_recv()
+        self.copy2(q, 1, b).wait_recv()
+        return self.l2[q, 0, b].astype(F32) + self.l2[q, 1, b].astype(F32)
 
     def run(self, finish):
         n = self.g.shape[2] // 2
@@ -291,26 +301,29 @@
                 for k in (0, 1):
                     a, b = self.block(q, first, 2 * d + k)
                     self.add((a, b, slice(None), self.cols(q)), self.l1[q, d, k])
-                self.copy2(q, d, 0).start()
-                self.copy2(q, d, 1).start()
+                far = self.order(q)[0]
+                low = jnp.where(far // 2 == d, far, 2 * d)
+                self.copy2(q, d, low).start()
+                self.copy2(q, d, 4 * d + 1 - low).start()
         for q in (0, 1):
             self.add(index(q, 0), self.arrived(q, 0))
             self.copy3(q, 0).start()
             self.copy3(q, 1).start()
-            for k in (2, 3):
-                self.copy2(q, 0, k).start()
-                self.copy2(q, 1, k).start()
         for d in (0, 1):
             for q in (0, 1):
                 self.add(index(q, 1 + d), self.arrived(q, 1 + d))
+                self.copy4(q, d, 1 - d).start()
+        for d in (0, 1):
+            for q in (0, 1):
                 a, b, _, cols = index(q, 1 + d)
                 self.copy3(q, d).wait_recv()
                 self.add((a, b, pl.ds(d * n, n), cols), self.l3[q, d])
-                self.copy4(q, d).start()
+                self.copy4(q, d, d).start()
         for q in (0, 1):
             value = self.g[index(q, 3)].astype(F32) + self.arrived(q, 3)
-            self.copy4(q, 0).wait_recv()
-            self.copy4(q, 1).wait_recv()
+            for d in (0, 1):
+                self.copy4(q, d, 0).wait_recv()
+                self.copy4(q, d, 1).wait_recv()
             finish(q, value + self.l4[q, 0].astype(F32) + self.l4[q, 1].astype(F32))
 
     def drain(self):
@@ -327,14 +340,18 @@
         o_layer_buf, coef, wantp, count_out, count_in, loss_out, loss_in, loss_sum, loss_land, head_out, head_land,
         loads, stored, relayed, frecv, brecv,
         gsent, grecv1, grecv2, dsent, dgot,
-        csend, crecv, lsend, lrecv, zsend, zrecv,
+        csend, crecv, lsend, lrecv, zsend, zrecv, hsend, hrecv,
         *scatter,
     ) = refs
-    layer_refs, layer_sems = scatter[:9], scatter[9:13]
-    head_refs, head_sems = scatter[13:22], scatter[22:26]
-    n_mb, rows, width = xin.shape
+    layer_refs, layer_sems = scatter[:9], scatter[9:14]
+    n_mb, rows, width = xout.shape
     rank = cin.shape[1]
     out_width = head.shape[1]
+    part = pl.ds(0, out_width)
+    head_refs = (
+        layer_refs[0].at[:, :, :, part], scatter[14], layer_refs[2].at[:, :, :, part], *scatter[15:21]
+    )
+    head_sems = scatter[21:26]
     tile = width // PIECES
     place = Place(sections)
     s, core, first, last = place.s, place.core, place.first, place.last
@@ -352,6 +369,11 @@
     for n in range(7):
         load(n).start()
     knock(place)
+
+    load(0).wait()
+    enter()
+    gather = Gather(place, shard, w, (gsent, grecv1, grecv2, dsent, dgot))
+    gather.begin()
 
     @pl.when(first)
     def _():
@@ -366,10 +388,6 @@
             xin[m] = lifted
             pin[m] = lifted[rank:].astype(F32)[0:1]
 
-    load(0).wait()
-    enter()
-    gather = Gather(place, shard, w, (gsent, grecv1, grecv2, dsent, dgot))
-    gather.begin()
     gather.run()
     for n in (4, 5, 6):
         load(n).wait()
@@ -430,65 +448,92 @@
 
     late = s >= sections // 2
 
-    @pl.when(late)
+    @pl.when(jnp.logical_and(late, jnp.logical_or(last, place.carrier)))
     def _():
         turned_into(wt, w)
 
-    def fcopy(m, j):
+    def onward(slot, end):
+        m = lax.rem(slot, n_mb)
+        away = jnp.logical_or(slot >= n_mb, jnp.logical_and(jnp.logical_not(place.middle), core == 0))
+        to_own = jnp.logical_and(away, end)
+        taker = jnp.where(to_own, 0, 1)
+        return taker, m + jnp.where(jnp.logical_and(away, jnp.logical_not(end)), n_mb, 0)
+
+    def relayed_copy(slot, j, forth):
+        to = place.nxt if forth else place.prv
+        taker, there = onward(slot, to == (sections - 1 if forth else 0))
+        device = {"dp": taker, "section": to}
+        recv = frecv if forth else brecv
+        kind = 0 if forth else 2
+        if j == PIECES:
+            landing = pin if forth else cpin
+            return remote(cpout.at[slot], landing.at[there], relayed.at[kind + 1], recv.at[there, 1], device)
         cols = pl.ds(j * tile, tile)
-        return remote(
-            xout.at[m, pl.ds(0, rank), cols], xin.at[m, pl.ds(0, rank), cols],
-            relayed.at[0], frecv.at[m, 0], {"section": place.nxt},
-        )
-
-    def fpcopy(m):
-        return remote(
-            pout.at[m], pin.at[m], relayed.at[1], frecv.at[m, 1], {"section": place.nxt}
-        )
-
-    def bcopy(m, j):
-        cols = pl.ds(j * tile, tile)
-        return remote(
-            cout.at[m, :, cols], cin.at[m, :, cols],
-            relayed.at[2], brecv.at[m, 0], {"section": place.prv},
-        )
-
-    def bpcopy(m):
-        return remote(
-            cpout.at[m], cpin.at[m], relayed.at[3], brecv.at[m, 1], {"section": place.prv}
-        )
-
-    def forward(m, span, sending):
-        @pl.when(jnp.logical_not(first))
-        def _():
-            for i in range(span):
-                ref = xin.at[m + i, pl.ds(0, rank)]
-                remote(ref, ref, relayed.at[0], frecv.at[m + i, 0], {"section": place.nxt}).wait_recv()
-                fpcopy(m + i).wait_recv()
-                xin[m + i, pl.ds(rank, rows - rank), :] = first_row(pin[m + i], rows - rank).astype(BF16)
-
+        landing = xin.at[there, pl.ds(0, rank), cols] if forth else cin.at[there, :, cols]
+        return remote(cout.at[slot, :, cols], landing, relayed.at[kind], recv.at[there, 0], device)
+
+    def await_relayed(slot, forth):
+        recv = frecv if forth else brecv
+        ref = xin.at[slot, pl.ds(0, rank)] if forth else cin.at[slot]
+        remote(ref, ref, relayed.at[0], recv.at[slot, 0], {"section": place.nxt}).wait_recv()
+        ref = pin.at[slot] if forth else cpin.at[slot]
+        remote(ref, ref, relayed.at[1], recv.at[slot, 1], {"section": place.nxt}).wait_recv()
+
+    def relays_left(forth):
+        kind = 0 if forth else 2
+        for count, when in ((n_mb, jnp.logical_not(place.middle)), (2 * n_mb, place.carrier)):
+
+            @pl.when(when)
+            def _(count=count):
+                for n, ref in ((kind, cin), (kind + 1, cpin)):
+                    ref = ref.at[pl.ds(0, count)]
+                    remote(ref, ref, relayed.at[n], frecv.at[0, 0], {"section": place.nxt}).wait_send()
+
+    def hand_over(kind, slot):
+        to = slot - n_mb
+        pairs = ((xin, pin), (mix, mixp))[kind]
+        for n, ref in enumerate(pairs):
+            sem = 2 * kind + n
+            remote(ref.at[slot], ref.at[to], hsend.at[sem], hrecv.at[sem], {"dp": 1 - core}).start()
+
+    def handed(kind):
+        pairs = ((xin, pin), (mix, mixp))[kind]
+        for n, ref in enumerate(pairs):
+            ref = ref.at[pl.ds(0, n_mb)]
+            sem = 2 * kind + n
+            yield remote(ref, ref, hsend.at[sem], hrecv.at[sem], {"dp": 1 - core})
+
+    def blocks(ref, slots):
+        return jnp.concatenate([ref[slot] for slot in slots], axis=0)
+
+    def forward(slots, arriving, sending):
+        if arriving:
+            for slot in slots:
+                await_relayed(slot, True)
+                xin[slot, pl.ds(rank, rows - rank), :] = first_row(pin[slot], rows - rank).astype(BF16)
         for j in range(PIECES):
             cols = pl.ds(j * tile, tile)
-            both = jnp.dot(
-                xin[pl.ds(m, span)].reshape(span * rows, width), w[:, cols], preferred_element_type=F32
-            )
-            for i in range(span):
+            both = jnp.dot(blocks(xin, slots), w[:, cols], preferred_element_type=F32)
+            for i, slot in enumerate(slots):
                 acc = both[i * rows : i * rows + rows]
                 th = jnp.tanh(acc[rank : rank + 1, :])
                 slope = 1.0 - th * th
                 tangent = acc[:rank, :]
-                pre[m + i, :, cols] = tangent
-                thb[m + i, :, cols] = th
-                moved = xin[m + i, pl.ds(0, rank), cols].astype(F32) + slope * tangent
-                xout[m + i, pl.ds(0, rank), cols] = moved.astype(BF16)
-                primal = (pin[m + i, :, cols] + th).astype(BF16).astype(F32)
-                pout[m + i, :, cols] = primal
-                xout[m + i, pl.ds(rank, rows - rank), cols] = first_row(primal, rows - rank).astype(BF16)
+                pre[slot, :, cols] = tangent.astype(BF16)
+                thb[slot, :, cols] = th
+                moved = xin[slot, pl.ds(0, rank), cols].astype(F32) + slope * tangent
+                primal = (pin[slot, :, cols] + th).astype(BF16).astype(F32)
                 if sending:
-                    fcopy(m + i, j).start()
+                    cout[slot, :, cols] = moved.astype(BF16)
+                    cpout[slot, :, cols] = primal
+                    relayed_copy(slot, j, True).start()
+                else:
+                    pout[slot, :, cols] = primal
+                    xout[slot, pl.ds(0, rank), cols] = moved.astype(BF16)
+                    xout[slot, pl.ds(rank, rows - rank), cols] = first_row(primal, rows - rank).astype(BF16)
         if sending:
-            for i in range(span):
-                fpcopy(m + i).start()
+            for slot in slots:
+                relayed_copy(slot, PIECES, True).start()
 
     def loss_copy(step):
         plane = 2 * chips
@@ -542,42 +587,38 @@
             th = thb[m, :, cols]
             slope = 1.0 - th * th
             mix[m, pl.ds(0, rank), cols] = (upstream * slope).astype(BF16)
-            total = jnp.sum(upstream * pre[m, :, cols], axis=0, keepdims=True)
+            total = jnp.sum(upstream * pre[m, :, cols].astype(F32), axis=0, keepdims=True)
             primal = cpin[m, :, cols] * slope - 2.0 * total * th * slope
             mixp[m, :, cols] = primal
             mix[m, pl.ds(rank, rows - rank), cols] = first_row(primal, rows - rank).astype(BF16)
 
-    def backward(m, span):
-        for i in range(span):
-            mixed(m + i)
-
-        @pl.when(jnp.logical_not(first))
-        def _():
-            for j in range(PIECES):
-                cols = pl.ds(j * tile, tile)
-                both = jnp.dot(
-                    mix[pl.ds(m, span)].reshape(span * rows, width), wt[:, cols],
-                    preferred_element_type=F32,
+    def backward(slots, together):
+        for j in range(PIECES):
+            cols = pl.ds(j * tile, tile)
+            both = jnp.dot(blocks(mix, slots), wt[:, cols], preferred_element_type=F32)
+            for i, slot in enumerate(slots):
+                back = both[i * rows : (i + 1) * rows]
+                cout[slot, :, cols] = (cin[slot, :, cols].astype(F32) + back[:rank]).astype(BF16)
+                cpout[slot, :, cols] = (
+                    (cpin[slot, :, cols] + back[rank : rank + 1]).astype(BF16).astype(F32)
                 )
-                for i in range(span):
-                    back = both[i * rows : (i + 1) * rows]
-                    cout[m + i, :, cols] = (cin[m + i, :, cols].astype(F32) + back[:rank]).astype(BF16)
-                    cpout[m + i, :, cols] = (
-                        (cpin[m + i, :, cols] + back[rank : rank + 1]).astype(BF16).astype(F32)
-                    )
-                bcopy(m, j).start()
-            bpcopy(m).start()
-            for i in range(1, span):
-                for j in range(PIECES):
-                    bcopy(m + i, j).start()
-                bpcopy(m + i).start()
+                if together or i == 0:
+                    relayed_copy(slot, j, False).start()
+        if together:
+            for slot in slots:
+                relayed_copy(slot, PIECES, False).start()
+        else:
+            relayed_copy(slots[0], PIECES, False).start()
+            for slot in slots[1:]:
+                for j in range(PIECES + 1):
+                    relayed_copy(slot, j, False).start()
 
     heads = Scatter(place, head_refs, head_sems)
     sums = Scatter(place, layer_refs, layer_sems)
 
     def compact(tangent, primal):
         def take(cols):
-            block = tangent[:, pl.ds(0, rank), cols]
+            block = tangent[pl.ds(0, n_mb), pl.ds(0, rank), cols]
             rest = stacked_rows(lambda m: primal[m, :, cols], n_mb, 16, block.shape[2])
             return jnp.concatenate(
                 [block.reshape(n_mb * rank, block.shape[2]), rest.astype(BF16)], axis=0
@@ -585,39 +626,83 @@
 
         return take
 
+    def each(count, body):
+        lax.fori_loop(0, count, lambda n, _: (body(n), 0)[1], 0)
+
     @pl.when(last)
     def _():
-        span = 2
-
-        def group(g, _):
-            forward(g * span, span, False)
-            objective(g * span, span)
-            backward(g * span, span)
-            return 0
-
-        lax.fori_loop(0, n_mb // span, group, 0)
+        def group(g):
+            slots = (2 * g, 2 * g + 1)
+            forward(slots, True, False)
+            objective(2 * g, 2)
+            for slot in slots:
+                mixed(slot)
+            backward(slots, False)
+
+        each(n_mb // 2, group)
         loss_in[core * chips + place.mp] = loss_out[...]
         lax.fori_loop(1, 2 * chips, lambda i, _: (loss_copy(i).start(), 0)[1], 0)
         sums.turn(compact(xin, pin))
 
-    @pl.when(jnp.logical_not(last))
-    def _():
-        lax.fori_loop(0, n_mb, lambda m, _: (forward(m, 1, True), 0)[1], 0)
-
-        @pl.when(jnp.logical_not(jnp.logical_or(late, first)))
+    @pl.when(first)
+    def _():
+        each(n_mb, lambda m: forward((m,), False, True))
+        sums.turn(compact(xin, pin))
+
+        def back(m):
+            await_relayed(m, False)
+            mixed(m)
+
+        each(n_mb, back)
+        relays_left(True)
+
+    @pl.when(place.carrier)
+    def _():
+        def slot_of(unit):
+            return unit // 2 + lax.rem(unit, 2) * n_mb
+
+        def forth(unit):
+            forward((slot_of(unit),), True, True)
+
+            @pl.when(lax.rem(unit, 2) == 1)
+            def _():
+                hand_over(0, slot_of(unit))
+
+        each(2 * n_mb, forth)
+
+        @pl.when(jnp.logical_not(late))
         def _():
             turned_into(wt, w)
 
+        @pl.when(jnp.logical_not(late))
+        def _():
+            sums.turn(compact(xin, pin))
+
+        relays_left(True)
+
+        def back(unit):
+            slot = slot_of(unit)
+            await_relayed(slot, False)
+            mixed(slot)
+            backward((slot,), True)
+
+            @pl.when(lax.rem(unit, 2) == 1)
+            def _():
+                hand_over(1, slot)
+
+        each(2 * n_mb, back)
+
+        @pl.when(late)
+        def _():
+            sums.turn(compact(xin, pin))
+
+    @pl.when(jnp.logical_and(place.middle, core == 0))
+    def _():
+        for copy in handed(0):
+            copy.wait_recv()
         sums.turn(compact(xin, pin))
-
-        def back(m, _):
-            ref = cin.at[m]
-            remote(ref, ref, relayed.at[2], brecv.at[m, 0], {"section": place.prv}).wait_recv()
-            bpcopy(m).wait_recv()
-            backward(m, 1)
-            return 0
-
-        lax.fori_loop(0, n_mb, back, 0)
+        for copy in handed(1):
+            copy.wait_recv()
 
     def section_copy(step, what):
         other = lax.rem(place.s + step, sections)
@@ -646,7 +731,8 @@
             return 0
 
         lax.fori_loop(1, sections, spread, 0)
-        o_head[...] = head_out[sections - 1]
+        heads.drain()
+        o_head[...] = head_out[sections - 1].astype(BF16)
         o_loss[...] = loss_sum[0:1, 0:1]
 
     sums.right[...] = compact(mix, mixp)(slice(None))
@@ -657,7 +743,7 @@
         return pltpu.make_async_copy(o_layer_buf.at[:, cols], o_layer.at[:, cols], stored.at[q])
 
     def finish_layer(q, value):
-        o_layer_buf[:, pl.ds(q * sums.half, sums.half)] = value
+        o_layer_buf[:, pl.ds(q * sums.half, sums.half)] = value.astype(BF16)
         layer_out(q).start()
 
     sums.run(finish_layer)
@@ -666,21 +752,18 @@
     def _():
         section_copy(1, 0).wait_recv()
         section_copy(1, 1).wait_recv()
-        o_head[...] = head_land[...]
+        o_head[...] = head_land[...].astype(BF16)
         o_loss[...] = loss_land[0:1, 0:1]
 
-    def relays_left(ref, n):
-        remote(ref, ref, relayed.at[n], frecv.at[0, 0], {"section": place.nxt}).wait_send()
-
-    @pl.when(jnp.logical_not(last))
-    def _():
-        relays_left(cin, 0)
-        relays_left(pout, 1)
-
     @pl.when(jnp.logical_not(first))
     def _():
-        relays_left(cout, 2)
-        relays_left(cpout, 3)
+        relays_left(False)
+
+    @pl.when(place.carrier)
+    def _():
+        for kind in (0, 1):
+            for copy in handed(kind):
+                copy.wait_send()
 
     gather.drain()
     sums.drain()
@@ -689,7 +772,6 @@
 
     @pl.when(last)
     def _():
-        heads.drain()
         all_counts().wait_send()
         all_losses().wait_send()
         for ref, n in ((head_out, 0), (loss_in, 1)):
@@ -697,21 +779,22 @@
             remote(ref, ref, zsend.at[n], zrecv.at[n], {"section": place.nxt}).wait_send()
 
 
-def scatter_scratch(rows, cols, depth):
+def scatter_scratch(rows, cols, depth, shared):
     half = cols // 2
     dma = pltpu.SemaphoreType.DMA
     part = (SIDE, SIDE, rows, cols)
+    local = [] if shared else [pltpu.VMEM(part, BF16)]
     return [
+        *local,
         pltpu.VMEM(part, BF16),
-        pltpu.VMEM(part, BF16),
-        pltpu.VMEM(part, BF16),
+        *local,
         pltpu.VMEM((2, 2, 2, rows, half), BF16),
         pltpu.VMEM((2, 2, SIDE, rows, half), BF16),
         pltpu.VMEM((2, 2, rows // 2, half), BF16),
         pltpu.VMEM((2, 2, rows, half), BF16),
         pltpu.VMEM((2, SIDE, SIDE, rows, depth), BF16),
         pltpu.VMEM((depth, cols), BF16),
-        dma((5,)), dma((2, SIDE)), dma((3, 2, 2)), dma((2, 2, SIDE)),
+        dma((5,)), dma((2, SIDE)), dma((2, 2, 2)), dma((2, 2, SIDE)), dma((2, 2, 2)),
     ]
 
 
@@ -730,13 +813,15 @@
     hbm = pl.BlockSpec(memory_space=pl.ANY)
     like = lambda a: pltpu.VMEM(a.shape, a.dtype)
     row = pltpu.VMEM((n_mb, 1, width), F32)
+    rows = pltpu.VMEM((2 * n_mb, 1, width), F32)
     block = pltpu.VMEM((n_mb, ROWS, width), BF16)
-    send = pltpu.VMEM((n_mb, rank, width), BF16)
+    blocks = pltpu.VMEM((2 * n_mb, ROWS, width), BF16)
+    send = pltpu.VMEM((2 * n_mb, rank, width), BF16)
     grad_layer, grad_head, loss = pl.pallas_call(
         functools.partial(step_kernel, sections, 1.0 / (lax.axis_size("dp") * n_mb * out_width)),
         out_shape=(
-            jax.ShapeDtypeStruct((own, width), F32),
-            jax.ShapeDtypeStruct((own, per), F32),
+            jax.ShapeDtypeStruct((own, width), BF16),
+            jax.ShapeDtypeStruct((own, per), BF16),
             jax.ShapeDtypeStruct((1, 1), F32),
         ),
         in_specs=[hbm] * 4 + [vmem] * 2 + [hbm] * 3,
@@ -747,13 +832,12 @@
             pltpu.VMEM((width, width), BF16),
             pltpu.VMEM((width, width), BF16),
             pltpu.VMEM((out_width, width), BF16),
-            block, block, block,
+            blocks, block, blocks,
             pltpu.VMEM((n_mb, ROWS, out_width), BF16),
-            row, row,
-            pltpu.VMEM((n_mb, rank, width), F32),
-            row, send, row, send, row, row,
+            rows, row, send,
+            rows, send, rows, send, rows, rows,
             pltpu.VMEM((n_mb, 1, out_width), F32),
-            pltpu.VMEM((own, width), F32),
+            pltpu.VMEM((own, width), BF16),
             pltpu.VMEM((n_mb, ROWS, 1), F32),
             pltpu.VMEM((n_mb, 1, out_width), F32),
             pltpu.VMEM((8, 128), F32),
@@ -764,11 +848,11 @@
             pltpu.VMEM((8, 128), F32),
             pltpu.VMEM((sections, own, per), F32),
             pltpu.VMEM((own, per), F32),
-            dma((7,)), dma((2,)), dma((4,)), dma((n_mb, 2)), dma((n_mb, 2)),
+            dma((7,)), dma((2,)), dma((4,)), dma((2 * n_mb, 2)), dma((2 * n_mb, 2)),
             dma, dma((2, 4)), dma((2, SIDE, 4)), dma, dma,
-            dma((1,)), dma((1,)), dma((1,)), dma((1,)), dma((2,)), dma((2,)),
-            *scatter_scratch(own, width, n_mb * rank + 16),
-            *scatter_scratch(own, out_width, n_mb * rank + 16),
+            dma((1,)), dma((1,)), dma((1,)), dma((1,)), dma((2,)), dma((2,)), dma((4,)), dma((4,)),
+            *scatter_scratch(own, width, n_mb * rank + 16, False),
+            *scatter_scratch(own, out_width, n_mb * rank + 16, True),
         ],
         compiler_params=pltpu.CompilerParams(
             collective_id=0, has_side_effects=True, vmem_limit_bytes=67043328
@@ -778,7 +862,7 @@
         inputs, tangents, targets, target_jac, rank_mask, batch_order, encoder, layers[0],
         head_weight,
     )
-    return grad_layer[None], grad_head, loss.reshape(())
+    return grad_layer[None].astype(F32), grad_head.astype(F32), loss.reshape(())
 
 
 def solution(mesh):

time: 172 us -> 168 us (0.977)
  Pallas kernels: 166 us -> 162 us
  local copies, waits for them, and re-layouts: 3.25 us -> 0 us
  other arithmetic: 0 us -> 3.11 us
    pallas_call x1, Pallas kernels: 166 us -> 162 us  [local(): pl.pallas_call(functools.partial(step_kernel, sections, 1.0 / (lax.axis_s...]
    unnamed x2 -> x0, local copies, waits for them, and re-layouts: 3.25 us -> none
    convert_element_type x0 -> x2, other arithmetic: none -> 3.11 us  [the longest x1 1.78 us: local(): grad_layer[None].astype(F32)]
where the time goes in v5:
time: 168 us; the launch traced here: 167 us
  Pallas kernels  162 us (96%)
  other arithmetic  3.11 us (2%)
  between operations  2.32 us (1%)
    pallas_call x1, Pallas kernels, local(): pl.pallas_call(functools.partial(step_kernel, sections, 1.0 / (lax.axis_s...  162 us

profile of v5, /device:TPU:1, one launch (start us, length us, event | category | flops | bytes accessed | tf_op | source)
XLA Modules:
  0.0 167.3 jit_solution(4786605575455775586)
XLA Ops:
  0.6 161.8 %step.1 = (bf16[64,2048]{1,0:T(8,128)(2,1)}, bf16[64,128]{1,0:T(8,128)(2,1)}, f32[1,1]{1,0:T(1,128)}) custom-call(bf16[6,512]{1,0:T(8,128)(2,1)} %refs_0_.1, bf16[6,32,512]{2,1,0:T(8,128)(2,1)} %refs_1_.1, bf16[6,1024]{1,0:T(8,128)(2,1)} %refs_2_.1, bf16[6,32,1024]{2,1,0:T(8,128)(2,1)} %refs_3_.1, s32[6,32]{1,0:T(8,128)} %refs_4_.1, s32[1,6]{1,0:T(1,128)} %refs_5_.1, ...), custom_call_target="tpu_custom_call" | custom-call | tf_op jit(solution)/shard_map/step/pallas_call | solution.py:820
  162.5 1.8 %bitcast_convert_fusion = f32[1,64,2048]{2,1,0:T(8,128)} fusion(bf16[64,2048]{1,0:T(8,128)(2,1)} %get-tuple-element.6), kind=kLoop, calls=%fused_computation | loop fusion | flops 131072 | bytes 786432 | tf_op jit(solution)/shard_map/convert_element_type | solution.py:865
  164.3 1.3 convert_element_type.11
